TPU v7x, 256 devices: a whole 4x4x8 slice. The times are simulated.
256 devices in a mesh: seq: 64 (over y, z, x_hi), tp: 4 (over x_lo, core).
Axes of the slice: x: 4 (x_hi: 2, x_lo: 2; x = x_hi * 2 + x_lo), y: 4, z: 8, core: 2. Of those that a mesh axis runs over, the one named last changes fastest.
Arguments:
- inputs: bfloat16 [8192, 2048], P(('seq', 'tp')), may hold values from -40 to 40
- gain: float32 [2048], replicated, may hold values from 0.5 to 1.5
- w_gate: bfloat16 [2048, 7168], P('seq', 'tp'), may hold values from -0.125 to 0.125
- w_up: bfloat16 [2048, 7168], P('seq', 'tp'), may hold values from -0.125 to 0.125
- grad_act: bfloat16 [8192, 7168], P('seq', 'tp'), may hold values from -12 to 12
Outputs:
- input_grad: bfloat16 [8192, 2048], P(('seq', 'tp'))
- gain_grad: float32 [2048], replicated
- gate_weight_grad: float32 [2048, 7168], P('seq', 'tp')
All inputs are finite; a program needn't handle non-finite values.
Results may differ from a plain program's by a relative error of at most 0.012.
Values may be sent and summed in bfloat16 or wider, within the bound.
No kernel may reach another device: no remote copies, remote signals or barrier semaphores. Data moves between devices by JAX's collectives and lax.ppermute only.
A program may use at most 128 MiB of HBM per device.

v0:
```python
import jax
import jax.numpy as jnp
from jax import lax
from jax.experimental import pallas as pl
from jax.experimental.pallas import tpu as pltpu
from jax.sharding import Mesh
from jax.sharding import PartitionSpec as P


SHAPE = (4, 2, 2, 2, 2, 2, 2)
AXES = ("y", "z1", "z0", "zv", "xh", "xl", "c")
TP = ("xl", "c")
SEQ = ("y", "z1", "z0", "zv", "xh")
SEQ_TP = SEQ + TP
Z = ("z1", "z0", "zv")
PLANE = ("y", "xh", "xl", "c")
SWAPPED = ("z1", "z0", "zv", "xh", "xl", "c")
HALF = 896
CUTS = ((0, 512), (512, 896))
CLASSES = (2, 4, 3, 12)
BF16, F32 = jnp.bfloat16, jnp.float32


def index_of(bits):
    value = 0
    for bit in bits:
        value = value * 2 + bit
    return value


def all_bits():
    for k in range(64):
        yield tuple((k >> (5 - j)) & 1 for j in range(6))


def pairs_of(there):
    return [(index_of(bits), index_of(there(*bits))) for bits in all_bits()]


def weight_pairs(m1, m0):
    return pairs_of(lambda z1, z0, zv, xh, xl, c: (c, xh ^ m0, xl, z0, z1, zv ^ m1))


def owner_pairs(m):
    return pairs_of(lambda z1, z0, zv, xh, xl, c: (c, xh ^ m, xl, z0, z1, zv))


def act_pairs(m):
    return pairs_of(lambda z1, z0, zv, xh, xl, c: (c, zv ^ m, xl, xh, z1, z0))


def row_pairs():
    return pairs_of(lambda z1, z0, zv, xh, xl, c: (zv, xl, c, xh, z1, z0))


def back(pairs):
    return [(b, a) for a, b in pairs]


def move(value, pairs):
    return lax.ppermute(value, SWAPPED, pairs)


def to_peer(value):
    return lax.ppermute(value, "c", [(0, 1), (1, 0)])


def class_of(core, color, stage):
    return CLASSES[(stage + 2 * core + color) % 4]


def exchange(value, color, stage):
    pairs = []
    for y in range(4):
        for xh in range(2):
            for xl in range(2):
                for c in range(2):
                    there = (y * 4 + xl * 2 + xh) ^ class_of(c, color, stage)
                    y2, xl2, xh2 = there // 4, (there // 2) % 2, there % 2
                    pairs.append(
                        (((y * 2 + xh) * 2 + xl) * 2 + c, ((y2 * 2 + xh2) * 2 + xl2) * 2 + c)
                    )
    return lax.ppermute(value, PLANE, pairs)


def tiles_in_order():
    core = lax.axis_index("c")
    here = lax.axis_index("y") * 4 + lax.axis_index("xl") * 2 + lax.axis_index("xh")
    flips = []
    for c in range(2):
        for color in range(2):
            for block in range(16):
                flip = 0
                for stage in range(4):
                    if (block >> stage) & 1:
                        flip ^= class_of(c, color, stage)
                flips.append(flip)
    first = jnp.array(flips, jnp.int32)
    second = jnp.array(flips[32:] + flips[:32], jnp.int32)
    return jnp.where(core == 1, second, first) ^ here.astype(jnp.int32)


def in_order(first, second, flag):
    return jnp.where(flag, second, first), jnp.where(flag, first, second)


def sent_to_all(value, axes):
    peers = lax.axis_size(axes)
    return lax.all_to_all(
        jnp.broadcast_to(value[None], (peers, *value.shape)), axes, 0, 0, tiled=True
    )


def flip_start(value, axes, flips):
    size = lax.axis_size(axes)
    return [lax.ppermute(value, axes, [(i, i ^ k) for i in range(size)]) for k in flips]


def flip_sum(value, arrived):
    terms = [value, *arrived]
    while len(terms) > 1:
        terms = [terms[k] + terms[k + 1] for k in range(0, len(terms), 2)]
    return terms[0]


def tile_at(tiles_ref, which, color, block):
    return tiles_ref[which * 32 + color * 16 + block]


def rows_kernel(rows_ref, gain_ref, normed_ref, turned_ref, inverse_ref):
    values = rows_ref[...].astype(F32)
    inverse = lax.rsqrt(jnp.mean(values * values, axis=-1, keepdims=True) + 1e-05)
    inverse_ref[...] = inverse
    for k in range(16):
        part = slice(k * 128, (k + 1) * 128)
        scaled = rows_ref[:, part].astype(F32) * inverse
        normed = (scaled * gain_ref[:, part]).astype(BF16)
        normed_ref[:, part] = normed
        turned_ref[part, :] = normed.T


def act_kernel(tiles_ref, core_ref, normed_ref, act_ref, rows_ref, inverse_ref, *refs):
    sources, (gate_ref, out_ref, terms_ref) = refs[:8], refs[8:11]
    weights, (ordered, mine, peer, total, sems) = refs[11:19], refs[19:]
    core = core_ref[0] == 1
    order = [which * 4 + color * 2 + part for color in (0, 1) for which in (0, 1) for part in (0, 1)]
    copies = {k: pltpu.make_async_copy(sources[k], weights[k], sems.at[k]) for k in order}
    for k in order:
        copies[k].start()
    for color, (low, high) in enumerate(CUTS):
        width = high - low
        found = []
        for which in range(2):
            for block in range(16):
                at = pl.multiple_of(tile_at(tiles_ref, which, color, block) * 128, 128)
                ordered[:, block * 128 : (block + 1) * 128] = normed_ref[:, pl.ds(at, 128)]
            sum_of = None
            for part in range(2):
                k = which * 4 + color * 2 + part
                copies[k].wait()
                term = jnp.dot(
                    ordered[:, part * 1024 : (part + 1) * 1024],
                    weights[k][...].reshape(1024, width),
                    preferred_element_type=F32,
                )
                sum_of = term if sum_of is None else sum_of + term
            found.append(sum_of)
        gate = jnp.where(core, found[1], found[0])
        up = jnp.where(core, found[0], found[1])
        sig = jax.nn.sigmoid(gate)
        cotangent = act_ref[:, low:high].astype(F32)
        d_up = (cotangent * gate * sig).astype(BF16)
        d_gate = (cotangent * up * sig * (1.0 + gate * (1.0 - sig))).astype(BF16)
        gate_ref[:, low:high] = d_gate
        mine[:, low:high] = jnp.where(core, d_up, d_gate)
        peer[:, low:high] = jnp.where(core, d_gate, d_up)
    total[...] = jnp.zeros_like(total)
    for which, d_ref in enumerate((mine, peer)):
        for color, (low, high) in enumerate(CUTS):
            for part in range(2):
                weight = weights[which * 4 + color * 2 + part][...].reshape(1024, high - low)
                found = lax.dot_general(
                    d_ref[:, low:high],
                    weight,
                    (((1,), (1,)), ((), ())),
                    preferred_element_type=F32,
                )
                for k in range(8):
                    tile = tile_at(tiles_ref, which, color, part * 8 + k)
                    at = pl.multiple_of(tile * 128, 128)
                    total[:, pl.ds(at, 128)] += found[:, k * 128 : (k + 1) * 128]
    for k in range(16):
        part = slice(k * 128, (k + 1) * 128)
        grad = total[:, part]
        out_ref[:, part] = grad.astype(BF16)
        scaled = rows_ref[:, part].astype(F32) * inverse_ref[...]
        terms_ref[:, part] = jnp.sum(grad * scaled, axis=0, keepdims=True)


def weight_grad_kernel(tiles_ref, core_ref, turned_ref, d_gate_ref, *refs):
    outs, (ordered,) = refs[:4], refs[4:]
    for which in range(2):
        half = (core_ref[0] + which) % 2
        for color, (low, high) in enumerate(CUTS):
            for block in range(16):
                tile = tile_at(tiles_ref, which, color, block)
                at = pl.multiple_of(tile * 128 + half * 64, 64)
                ordered[block * 64 : (block + 1) * 64, :] = turned_ref[pl.ds(at, 64), :]
            found = jnp.dot(ordered[...], d_gate_ref[:, low:high], preferred_element_type=F32)
            outs[which * 2 + color][...] = found.astype(BF16).reshape(16, 64, high - low)


def in_vmem(count):
    return [pl.BlockSpec(memory_space=pltpu.VMEM)] * count


def in_smem(count):
    return [pl.BlockSpec(memory_space=pltpu.SMEM)] * count


def local_call(kernel, shapes, scratch, scalars, arrays, flops, anywhere=()):
    return pl.pallas_call(
        kernel,
        out_shape=[jax.ShapeDtypeStruct(*shape) for shape in shapes],
        in_specs=in_smem(len(scalars))
        + in_vmem(len(arrays))
        + [pl.BlockSpec(memory_space=pl.ANY)] * len(anywhere),
        out_specs=in_vmem(len(shapes)),
        scratch_shapes=scratch,
        cost_estimate=pl.CostEstimate(flops=flops, bytes_accessed=8 << 20, transcendentals=0),
    )(*scalars, *arrays, *anywhere)


def step(inputs, gain, w_gate, w_up, grad_act):
    core_index = lax.axis_index("c")
    core = core_index == 1
    mid = lax.axis_index("z0") == 1
    low = lax.axis_index("zv") == 1
    high = lax.axis_index("xh") == 1
    tiles = tiles_in_order()
    cores = core_index.astype(jnp.int32).reshape(1)

    gates = in_order(w_gate[:, :HALF], w_gate[:, HALF:], high)
    ups = in_order(w_up[:, :HALF], w_up[:, HALF:], high)
    got = [[None, None], [None, None]]
    for m0 in range(2):
        for m1, piece in enumerate(in_order(gates[m0], ups[m0], low)):
            got[m1][m0] = move(piece, weight_pairs(m1, m0))
    own_inputs = move(inputs, row_pairs())
    sent = in_order(grad_act[:, :HALF], grad_act[:, HALF:], low)
    got_act = []
    for m in range(2):
        got_act.append(move(sent[m], act_pairs(m)))

    by_pair = [jnp.concatenate(in_order(*got[m1], mid), axis=0) for m1 in range(2)]
    piece = jnp.concatenate(in_order(*by_pair, core), axis=0)

    weights = [None] * 8
    held = [piece[None, :, a:b] for a, b in CUTS]
    for stage in range(4):
        arrived = []
        for color in range(2):
            arrived.append(exchange(held[color], color, stage))
        arrived = lax.optimization_barrier(arrived)
        if stage < 3:
            held = [jnp.concatenate((held[k], arrived[k]), axis=0) for k in range(2)]
        else:
            for color in range(2):
                for part, value in enumerate((held[color], arrived[color])):
                    weights[color * 2 + part] = value
                    weights[4 + color * 2 + part] = to_peer(value)

    rows = sent_to_all(own_inputs, Z).reshape(256, 2048)
    normed, turned, inverse = local_call(
        rows_kernel,
        [((256, 2048), BF16), ((2048, 256), BF16), ((256, 1), F32)],
        [],
        (),
        (rows, gain.reshape(1, 2048)),
        256 * 2048 * 64,
    )
    act = jnp.concatenate(in_order(got_act[0], got_act[1], mid), axis=0)

    d_gate, partial_grad, terms = local_call(
        act_kernel,
        [((256, HALF), BF16), ((256, 2048), BF16), ((1, 2048), F32)],
        [
            pltpu.VMEM((8, 128, b - a), BF16)
            for a, b in (CUTS[0], CUTS[0], CUTS[1], CUTS[1]) * 2
        ]
        + [
            pltpu.VMEM((256, 2048), BF16),
            pltpu.VMEM((256, HALF), BF16),
            pltpu.VMEM((256, HALF), BF16),
            pltpu.VMEM((256, 2048), F32),
            pltpu.SemaphoreType.DMA((8,)),
        ],
        (tiles, cores),
        (normed, act, rows, inverse),
        8 * 256 * 2048 * HALF,
        weights,
    )
    parts = lax.all_to_all(partial_grad.reshape(8, 32, 2048), Z, 0, 0, tiled=True)

    terms = terms.reshape(2048)
    terms = flip_sum(terms, flip_start(terms, "c", (1,)))
    grads = local_call(
        weight_grad_kernel,
        [((16, 64, b - a), BF16) for a, b in CUTS + CUTS],
        [pltpu.VMEM((1024, 256), BF16)],
        (tiles, cores),
        (turned, d_gate),
        4 * 256 * 2048 * HALF,
    )
    arrived = [to_peer(grads[2 + k]) for k in range(2)]
    flips = flip_start(terms, "xl", (1,))
    *arrived, flipped = lax.optimization_barrier((*arrived, *flips))
    terms = flip_sum(terms, [flipped])
    summed = [grads[k].astype(F32) + arrived[k].astype(F32) for k in range(2)]
    beside = {3: ("y", (1, 2, 3)), 2: ("xh", (1,)), 1: ("zv", (1,)), 0: ("z0", (1,))}
    for stage in (3, 2, 1, 0):
        count = 1 << stage
        going = [total.astype(BF16) for total in summed]
        arrived = [exchange(going[k][count:], k, stage) for k in range(2)]
        flips = flip_start(terms, *beside[stage])
        (*arrived,), (*flips,) = lax.optimization_barrier((tuple(arrived), tuple(flips)))
        terms = flip_sum(terms, flips)
        summed = [summed[k][:count] + arrived[k].astype(F32) for k in range(2)]
    own_rows = jnp.concatenate([total[0].astype(BF16) for total in summed], axis=1)
    sent = in_order(own_rows[:32], own_rows[32:], mid)
    got = [move(sent[m], back(owner_pairs(m))) for m in range(2)]
    gate_weight_grad = jnp.concatenate(in_order(got[0], got[1], high), axis=1).astype(F32)
    gain_grad = flip_sum(terms, flip_start(terms, "z1", (1,)))

    own_grad = parts.astype(F32).sum(axis=0)
    own_values = own_inputs.astype(F32)
    own_inverse = lax.rsqrt(jnp.mean(own_values * own_values, axis=-1, keepdims=True) + 1e-05)
    own_scaled = own_values * own_inverse
    gained = own_grad * gain
    middle = jnp.mean(gained * own_scaled, axis=-1, keepdims=True)
    own_input_grad = (own_inverse * (gained - own_scaled * middle)).astype(BF16)
    input_grad = move(own_input_grad, back(row_pairs()))
    return (input_grad, gain_grad, gate_weight_grad)


def solution(mesh):
    torus = Mesh(mesh.devices.reshape(SHAPE), AXES)
    placed = (P(SEQ_TP, None), P(), P(SEQ, TP), P(SEQ, TP), P(SEQ, TP))
    return jax.shard_map(
        step,
        mesh=torus,
        in_specs=placed,
        out_specs=(P(SEQ_TP, None), P(), P(SEQ, TP)),
        check_vma=False,
    )
```

profile of v0, /device:TPU:1, one launch (start us, length us, event | category | flops | bytes accessed | tf_op | source)
XLA Modules:
  0.0 208.5 jit_solution(809256274342385088)
XLA Ops:
  1.6 6.9 %collective-permute-start.3 = (bf16[32,896]{1,0:T(8,128)(2,1)S(1)}, bf16[32,896]{1,0:T(8,128)(2,1)S(1)}, u32[]{:S(2)}, u32[]{:S(2)}) collective-permute-start(bf16[32,896]{1,0:T(8,128)(2,1)S(1)} %get-tuple-element.79), channel_id=1, source_target_pairs={{0,17},{1,49},{2,25},{3,57},{4,1},{5,33},{6,9},{7,41},{8,16},{9,48... | collective-permute-start | bytes 172040 | tf_op jit(solution)/shard_map/ppermute | solution.py:61
  8.5 3.0 %collective-permute-start.4 = (bf16[32,896]{1,0:T(8,128)(2,1)S(1)}, bf16[32,896]{1,0:T(8,128)(2,1)S(1)}, u32[]{:S(2)}, u32[]{:S(2)}) collective-permute-start(bf16[32,896]{1,0:T(8,128)(2,1)S(1)} %get-tuple-element.80), channel_id=1, source_target_pairs={{0,1},{1,33},{2,9},{3,41},{4,17},{5,49},{6,25},{7,57},{8,0},{9,32}... | collective-permute-start | bytes 172040 | tf_op jit(solution)/shard_map/ppermute | solution.py:61
  11.5 3.4 %collective-permute-start.5 = (bf16[32,896]{1,0:T(8,128)(2,1)S(1)}, bf16[32,896]{1,0:T(8,128)(2,1)S(1)}, u32[]{:S(2)}, u32[]{:S(2)}) collective-permute-start(bf16[32,896]{1,0:T(8,128)(2,1)S(1)} %get-tuple-element.81), channel_id=1, source_target_pairs={{0,16},{1,48},{2,24},{3,56},{4,0},{5,32},{6,8},{7,40},{8,17},{9,49... | collective-permute-start | bytes 172040 | tf_op jit(solution)/shard_map/ppermute | solution.py:61
  14.9 4.0 %collective-permute-start.6 = (bf16[32,896]{1,0:T(8,128)(2,1)S(1)}, bf16[32,896]{1,0:T(8,128)(2,1)S(1)}, u32[]{:S(2)}, u32[]{:S(2)}) collective-permute-start(bf16[32,896]{1,0:T(8,128)(2,1)S(1)} %get-tuple-element.82), channel_id=1, source_target_pairs={{0,0},{1,32},{2,8},{3,40},{4,16},{5,48},{6,24},{7,56},{8,1},{9,33}... | collective-permute-start | bytes 172040 | tf_op jit(solution)/shard_map/ppermute | solution.py:61
  20.5 4.7 %collective-permute-start.7 = (bf16[1,128,512]{2,1,0:T(8,128)(2,1)S(1)}, bf16[1,128,512]{2,1,0:T(8,128)(2,1)S(1)}, u32[]{:S(2)}, u32[]{:S(2)}) collective-permute-start(bf16[1,128,512]{2,1,0:T(8,128)(2,1)S(1)} %fusion.8), channel_id=1, source_target_pairs={{0,2},{1,7},{2,0},{3,5},{4,6},{5,3},{6,4},{7,1},{64,66},{65,71},{6... | collective-permute-start | bytes 393224 | tf_op jit(solution)/shard_map/ppermute | solution.py:83
  25.2 2.8 %collective-permute-start.8 = (bf16[1,128,384]{2,1,0:T(8,128)(2,1)S(1)}, bf16[1,128,384]{2,1,0:T(8,128)(2,1)S(1)}, u32[]{:S(2)}, u32[]{:S(2)}) collective-permute-start(bf16[1,128,384]{2,1,0:T(8,128)(2,1)S(1)} %fusion.11), channel_id=1, source_target_pairs={{0,64},{1,193},{2,66},{3,195},{4,68},{5,197},{6,70},{7,199},{64,0}... | collective-permute-start | bytes 294920 | tf_op jit(solution)/shard_map/ppermute | solution.py:83
  30.1 2.8 %collective-permute-start.9 = (bf16[2,128,512]{2,1,0:T(8,128)(2,1)S(1)}, bf16[2,128,512]{2,1,0:T(8,128)(2,1)S(1)}, u32[]{:S(2)}, u32[]{:S(2)}) collective-permute-start(bf16[2,128,512]{2,1,0:T(8,128)(2,1)S(1)} %pad_maximum_fusion.5), channel_id=1, source_target_pairs={{0,64},{1,193},{2,66},{3,195},{4,68},{5,197},{6,70},{7,199},{64,0}... | collective-permute-start | bytes 786440 | tf_op jit(solution)/shard_map/ppermute | solution.py:83
  34.6 3.1 %collective-permute-done.10 = bf16[2,128,384]{2,1,0:T(8,128)(2,1)S(1)} collective-permute-done((bf16[2,128,384]{2,1,0:T(8,128)(2,1)S(1)}, bf16[2,128,384]{2,1,0:T(8,128)(2,1)S(1)}, u32[]{:S(2)}, u32[]{:S(2)}) %collective-permute-start.10) | collective-permute-done | bytes 196640 | tf_op jit(solution)/shard_map/ppermute | solution.py:83
  39.4 6.9 %collective-permute-done.12 = bf16[4,128,384]{2,1,0:T(8,128)(2,1)S(1)} collective-permute-done((bf16[4,128,384]{2,1,0:T(8,128)(2,1)S(1)}, bf16[4,128,384]{2,1,0:T(8,128)(2,1)S(1)}, u32[]{:S(2)}, u32[]{:S(2)}) %collective-permute-start.12) | collective-permute-done | bytes 393248 | tf_op jit(solution)/shard_map/ppermute | solution.py:83
  46.6 7.6 %collective-permute-start = (bf16[32,2048]{1,0:T(8,128)(2,1)S(1)}, bf16[32,2048]{1,0:T(8,128)(2,1)S(1)}, u32[]{:S(2)}, u32[]{:S(2)}) collective-permute-start(bf16[32,2048]{1,0:T(8,128)(2,1)S(1)} %copy-done.10), channel_id=1, source_target_pairs={{0,0},{1,8},{2,16},{3,24},{4,4},{5,12},{6,20},{7,28},{8,32},{9,40}... | collective-permute-start | bytes 393224 | tf_op jit(solution)/shard_map/ppermute | solution.py:61
  56.3 3.3 %collective-permute-done = bf16[32,2048]{1,0:T(8,128)(2,1)S(1)} collective-permute-done((bf16[32,2048]{1,0:T(8,128)(2,1)S(1)}, bf16[32,2048]{1,0:T(8,128)(2,1)S(1)}, u32[]{:S(2)}, u32[]{:S(2)}) %collective-permute-start) | collective-permute-done | bytes 131104 | tf_op jit(solution)/shard_map/ppermute | solution.py:61
  60.8 3.6 %all-to-all-start = ((bf16[8,32,2048]{2,1,0:T(8,128)(2,1)}), bf16[8,32,2048]{2,1,0:T(8,128)(2,1)S(1)}, u32[]{:S(2)}, u32[]{:S(2)}) async-start(bf16[8,32,2048]{2,1,0:T(8,128)(2,1)} %broadcast_in_dim.6), calls=%async_computation | async-start | bytes 2097152 | tf_op jit(solution)/shard_map/all_to_all | solution.py:109
  64.3 6.0 %collective-permute-start.15 = (bf16[8,128,512]{2,1,0:T(8,128)(2,1)S(1)}, bf16[8,128,512]{2,1,0:T(8,128)(2,1)}, u32[]{:S(2)}, u32[]{:S(2)}) collective-permute-start(bf16[8,128,512]{2,1,0:T(8,128)(2,1)S(1)} %pad_maximum_fusion.refs_0_), channel_id=1, source_target_pairs={{0,1},{1,0},{2,3},{3,2},{4,5},{5,4},{6,7},{7,6},{8,9},{9,8},{10,11... | collective-permute-start | bytes 3145736 | tf_op jit(solution)/shard_map/ppermute | solution.py:65
  71.2 4.0 %collective-permute-start.1 = (bf16[128,896]{1,0:T(8,128)(2,1)S(1)}, bf16[128,896]{1,0:T(8,128)(2,1)S(1)}, u32[]{:S(2)}, u32[]{:S(2)}) collective-permute-start(bf16[128,896]{1,0:T(8,128)(2,1)S(1)} %get-tuple-element.75), channel_id=1, source_target_pairs={{0,16},{1,48},{2,24},{3,56},{4,20},{5,52},{6,28},{7,60},{8,0},{9,3... | collective-permute-start | bytes 688136 | tf_op jit(solution)/shard_map/ppermute | solution.py:61
  75.7 20.6 %collective-permute-done.1 = bf16[128,896]{1,0:T(8,128)(2,1)S(1)} collective-permute-done((bf16[128,896]{1,0:T(8,128)(2,1)S(1)}, bf16[128,896]{1,0:T(8,128)(2,1)S(1)}, u32[]{:S(2)}, u32[]{:S(2)}) %collective-permute-start.1) | collective-permute-done | bytes 229408 | tf_op jit(solution)/shard_map/ppermute | solution.py:61
  96.4 6.8 %collective-permute-start.2 = (bf16[128,896]{1,0:T(8,128)(2,1)}, bf16[128,896]{1,0:T(8,128)(2,1)S(1)}, u32[]{:S(2)}, u32[]{:S(2)}) collective-permute-start(bf16[128,896]{1,0:T(8,128)(2,1)} %get-tuple-element.76), channel_id=1, source_target_pairs={{0,0},{1,32},{2,8},{3,40},{4,4},{5,36},{6,12},{7,44},{8,16},{9,48}... | collective-permute-start | bytes 688136 | tf_op jit(solution)/shard_map/ppermute | solution.py:61
  103.8 2.5 %collective-permute-done.2 = bf16[128,896]{1,0:T(8,128)(2,1)S(1)} collective-permute-done((bf16[128,896]{1,0:T(8,128)(2,1)}, bf16[128,896]{1,0:T(8,128)(2,1)S(1)}, u32[]{:S(2)}, u32[]{:S(2)}) %collective-permute-start.2) | collective-permute-done | bytes 229408 | tf_op jit(solution)/shard_map/ppermute | solution.py:61
  108.1 3.2 %shard_map.94 = (bf16[256,2048]{1,0:T(8,128)(2,1)}, bf16[2048,256]{1,0:T(8,128)(2,1)}, f32[256,1]{1,0:T(8,128)}) custom-call(bf16[256,2048]{1,0:T(8,128)(2,1)} %bitcast.13, f32[1,2048]{1,0:T(1,128)} %bitcast.16), custom_call_target="tpu_custom_call" | custom-call | flops 33554432 | bytes 8388608 | tf_op jit(solution)/shard_map/pallas_call | solution.py:222
  111.3 12.7 %shard_map.95 = (bf16[256,896]{1,0:T(8,128)(2,1)}, bf16[256,2048]{1,0:T(8,128)(2,1)}, f32[1,2048]{1,0:T(1,128)}) custom-call(s32[64]{0:T(128)} %fusion.15.tiles_ref, s32[1]{0:T(128)} %bitcast.core_ref, bf16[256,2048]{1,0:T(8,128)(2,1)} %get-tuple-element.38.normed_ref, bf16[256,896]{1,0:T(8,128)(2,1)} %pad_maximum_fusion.3.act_ref, ...), custom_call_target="tpu_custom_call" | custom-call | flops 3758096384 | bytes 8388608 | tf_op jit(solution)/shard_map/pallas_call | solution.py:222
  124.0 4.2 %shard_map.96 = (bf16[16,64,512]{2,1,0:T(8,128)(2,1)}, bf16[16,64,384]{2,1,0:T(8,128)(2,1)}, bf16[16,64,512]{2,1,0:T(8,128)(2,1)}, bf16[16,64,384]{2,1,0:T(8,128)(2,1)}) custom-call(s32[64]{0:T(128)} %fusion.15.tiles_ref, s32[1]{0:T(128)} %bitcast.core_ref, bf16[2048,256]{1,0:T(8,128)(2,1)} %get-tuple-element.50.turned_ref, ...), custom_call_target="tpu_custom_call" | custom-call | flops 1879048192 | bytes 8388608 | tf_op jit(solution)/shard_map/pallas_call | solution.py:222
  128.7 3.5 %collective-permute-done.20 = f32[2048]{0:T(1024)S(1)} collective-permute-done((f32[2048]{0:T(1024)S(1)}, f32[2048]{0:T(1024)S(1)}, u32[]{:S(2)}, u32[]{:S(2)}) %collective-permute-start.20) | collective-permute-done | bytes 8224 | tf_op jit(solution)/shard_map/ppermute | solution.py:116
  132.2 7.8 %collective-permute-start.23 = (f32[2048]{0:T(1024)S(1)}, f32[2048]{0:T(1024)S(1)}, u32[]{:S(2)}, u32[]{:S(2)}) collective-permute-start(f32[2048]{0:T(1024)S(1)} %add.78), channel_id=1, source_target_pairs={{0,2},{2,0},{1,3},{3,1},{4,6},{6,4},{5,7},{7,5},{8,10},{10,8},{9,1... | collective-permute-start | bytes 24584 | tf_op jit(solution)/shard_map/ppermute | solution.py:116
  146.8 6.8 %all-to-all-start.1 = ((bf16[8,32,2048]{2,1,0:T(8,128)(2,1)}), bf16[8,32,2048]{2,1,0:T(8,128)(2,1)S(1)}, u32[]{:S(2)}, u32[]{:S(2)}) async-start(bf16[8,32,2048]{2,1,0:T(8,128)(2,1)} %bitcast.15), calls=%async_computation.1 | async-start | bytes 2097152 | tf_op jit(solution)/shard_map/all_to_all | solution.py:303
  155.4 2.2 %collective-permute-start.28 = (f32[2048]{0:T(1024)S(1)}, f32[2048]{0:T(1024)S(1)}, u32[]{:S(2)}, u32[]{:S(2)}) collective-permute-start(f32[2048]{0:T(1024)S(1)} %add.79), channel_id=1, source_target_pairs={{0,192},{64,128},{128,64},{192,0},{1,193},{65,129},{129,65},{193,1... | collective-permute-start | bytes 24584 | tf_op jit(solution)/shard_map/ppermute | solution.py:116
  163.0 2.5 %collective-permute-start.31 = (f32[2048]{0:T(1024)S(1)}, f32[2048]{0:T(1024)S(1)}, u32[]{:S(2)}, u32[]{:S(2)}) collective-permute-start(f32[2048]{0:T(1024)S(1)} %add_add_fusion), channel_id=1, source_target_pairs={{0,4},{4,0},{1,5},{5,1},{2,6},{6,2},{3,7},{7,3},{8,12},{12,8},{9,1... | collective-permute-start | bytes 24584 | tf_op jit(solution)/shard_map/ppermute | solution.py:116
  165.5 4.1 %collective-permute-done.31 = f32[2048]{0:T(1024)S(1)} collective-permute-done((f32[2048]{0:T(1024)S(1)}, f32[2048]{0:T(1024)S(1)}, u32[]{:S(2)}, u32[]{:S(2)}) %collective-permute-start.31) | collective-permute-done | bytes 8224 | tf_op jit(solution)/shard_map/ppermute | solution.py:116
  173.7 6.0 %all-to-all-done.1 = bf16[8,32,2048]{2,1,0:T(8,128)(2,1)S(1)} async-done(((bf16[8,32,2048]{2,1,0:T(8,128)(2,1)}), bf16[8,32,2048]{2,1,0:T(8,128)(2,1)S(1)}, u32[]{:S(2)}, u32[]{:S(2)}) %all-to-all-start.1) | async-done | bytes 1048608 | tf_op jit(solution)/shard_map/all_to_all | solution.py:303
  180.3 5.9 %collective-permute-start.35 = (bf16[1,64,512]{2,1,0:T(8,128)(2,1)S(1)}, bf16[1,64,512]{2,1,0:T(8,128)(2,1)S(1)}, u32[]{:S(2)}, u32[]{:S(2)}) collective-permute-start(bf16[1,64,512]{2,1,0:T(8,128)(2,1)S(1)} %slice.220), channel_id=1, source_target_pairs={{0,2},{1,7},{2,0},{3,5},{4,6},{5,3},{6,4},{7,1},{64,66},{65,71},{6... | collective-permute-start | bytes 196616 | tf_op jit(solution)/shard_map/ppermute | solution.py:83
  186.3 5.0 %collective-permute-start.19 = (bf16[32,2048]{1,0:T(8,128)(2,1)S(1)}, bf16[32,2048]{1,0:T(8,128)(2,1)S(1)}, u32[]{:S(2)}, u32[]{:S(2)}) collective-permute-start(bf16[32,2048]{1,0:T(8,128)(2,1)S(1)} %fusion.5), channel_id=1, source_target_pairs={{0,0},{8,1},{16,2},{24,3},{4,4},{12,5},{20,6},{28,7},{32,8},{40,9}... | collective-permute-start | bytes 393224 | tf_op jit(solution)/shard_map/ppermute | solution.py:61
  191.4 2.6 %collective-permute-start.39 = (bf16[32,896]{1,0:T(8,128)(2,1)S(1)}, bf16[32,896]{1,0:T(8,128)(2,1)S(1)}, u32[]{:S(2)}, u32[]{:S(2)}) collective-permute-start(bf16[32,896]{1,0:T(8,128)(2,1)S(1)} %get-tuple-element.85), channel_id=1, source_target_pairs={{16,0},{48,1},{24,2},{56,3},{0,4},{32,5},{8,6},{40,7},{17,8},{49,9... | collective-permute-start | bytes 172040 | tf_op jit(solution)/shard_map/ppermute | solution.py:61
  194.1 5.9 %collective-permute-start.40 = (bf16[32,896]{1,0:T(8,128)(2,1)S(1)}, bf16[32,896]{1,0:T(8,128)(2,1)S(1)}, u32[]{:S(2)}, u32[]{:S(2)}) collective-permute-start(bf16[32,896]{1,0:T(8,128)(2,1)S(1)} %get-tuple-element.86), channel_id=1, source_target_pairs={{0,0},{32,1},{8,2},{40,3},{16,4},{48,5},{24,6},{56,7},{1,8},{33,9}... | collective-permute-start | bytes 172040 | tf_op jit(solution)/shard_map/ppermute | solution.py:61
  200.1 6.4 %collective-permute-done.38 = f32[2048]{0:T(1024)S(1)} collective-permute-done((f32[2048]{0:T(1024)S(1)}, f32[2048]{0:T(1024)S(1)}, u32[]{:S(2)}, u32[]{:S(2)}) %collective-permute-start.38) | collective-permute-done | bytes 8224 | tf_op jit(solution)/shard_map/ppermute | solution.py:116
  (131 shorter events, 36.5 us)
Async XLA Ops:
  1.6 17.4 %collective-permute-start.3 = (bf16[32,896]{1,0:T(8,128)(2,1)S(1)}, bf16[32,896]{1,0:T(8,128)(2,1)S(1)}, u32[]{:S(2)}, u32[]{:S(2)}) collective-permute-start(bf16[32,896]{1,0:T(8,128)(2,1)S(1)} %get-tuple-element.79), channel_id=1, source_target_pairs={{0,17},{1,49},{2,25},{3,57},{4,1},{5,33},{6,9},{7,41},{8,16},{9,48... | collective-permute-start | bytes 172040 | tf_op jit(solution)/shard_map/ppermute | solution.py:61
  8.5 10.5 %collective-permute-start.4 = (bf16[32,896]{1,0:T(8,128)(2,1)S(1)}, bf16[32,896]{1,0:T(8,128)(2,1)S(1)}, u32[]{:S(2)}, u32[]{:S(2)}) collective-permute-start(bf16[32,896]{1,0:T(8,128)(2,1)S(1)} %get-tuple-element.80), channel_id=1, source_target_pairs={{0,1},{1,33},{2,9},{3,41},{4,17},{5,49},{6,25},{7,57},{8,0},{9,32}... | collective-permute-start | bytes 172040 | tf_op jit(solution)/shard_map/ppermute | solution.py:61
  11.5 7.5 %collective-permute-start.5 = (bf16[32,896]{1,0:T(8,128)(2,1)S(1)}, bf16[32,896]{1,0:T(8,128)(2,1)S(1)}, u32[]{:S(2)}, u32[]{:S(2)}) collective-permute-start(bf16[32,896]{1,0:T(8,128)(2,1)S(1)} %get-tuple-element.81), channel_id=1, source_target_pairs={{0,16},{1,48},{2,24},{3,56},{4,0},{5,32},{6,8},{7,40},{8,17},{9,49... | collective-permute-start | bytes 172040 | tf_op jit(solution)/shard_map/ppermute | solution.py:61
  20.5 9.5 %collective-permute-start.7 = (bf16[1,128,512]{2,1,0:T(8,128)(2,1)S(1)}, bf16[1,128,512]{2,1,0:T(8,128)(2,1)S(1)}, u32[]{:S(2)}, u32[]{:S(2)}) collective-permute-start(bf16[1,128,512]{2,1,0:T(8,128)(2,1)S(1)} %fusion.8), channel_id=1, source_target_pairs={{0,2},{1,7},{2,0},{3,5},{4,6},{5,3},{6,4},{7,1},{64,66},{65,71},{6... | collective-permute-start | bytes 393224 | tf_op jit(solution)/shard_map/ppermute | solution.py:83
  30.1 7.6 %collective-permute-start.9 = (bf16[2,128,512]{2,1,0:T(8,128)(2,1)S(1)}, bf16[2,128,512]{2,1,0:T(8,128)(2,1)S(1)}, u32[]{:S(2)}, u32[]{:S(2)}) collective-permute-start(bf16[2,128,512]{2,1,0:T(8,128)(2,1)S(1)} %pad_maximum_fusion.5), channel_id=1, source_target_pairs={{0,64},{1,193},{2,66},{3,195},{4,68},{5,197},{6,70},{7,199},{64,0}... | collective-permute-start | bytes 786440 | tf_op jit(solution)/shard_map/ppermute | solution.py:83
  37.7 8.6 %collective-permute-start.11 = (bf16[4,128,512]{2,1,0:T(8,128)(2,1)S(1)}, bf16[4,128,512]{2,1,0:T(8,128)(2,1)S(1)}, u32[]{:S(2)}, u32[]{:S(2)}) collective-permute-start(bf16[4,128,512]{2,1,0:T(8,128)(2,1)S(1)} %pad_maximum_fusion.2), channel_id=1, source_target_pairs={{0,6},{1,3},{2,4},{3,1},{4,2},{5,7},{6,0},{7,5},{64,70},{65,67},{6... | collective-permute-start | bytes 1572872 | tf_op jit(solution)/shard_map/ppermute | solution.py:83
  46.5 23.9 %collective-permute-start.13 = (bf16[8,128,512]{2,1,0:T(8,128)(2,1)S(1)}, bf16[8,128,512]{2,1,0:T(8,128)(2,1)}, u32[]{:S(2)}, u32[]{:S(2)}) collective-permute-start(bf16[8,128,512]{2,1,0:T(8,128)(2,1)S(1)} %pad_maximum_fusion.refs_0_), channel_id=1, source_target_pairs={{0,192},{1,65},{2,194},{3,67},{4,196},{5,69},{6,198},{7,71},{64,12... | collective-permute-start | bytes 3145736 | tf_op jit(solution)/shard_map/ppermute | solution.py:83
  46.6 13.0 %collective-permute-start = (bf16[32,2048]{1,0:T(8,128)(2,1)S(1)}, bf16[32,2048]{1,0:T(8,128)(2,1)S(1)}, u32[]{:S(2)}, u32[]{:S(2)}) collective-permute-start(bf16[32,2048]{1,0:T(8,128)(2,1)S(1)} %copy-done.10), channel_id=1, source_target_pairs={{0,0},{1,8},{2,16},{3,24},{4,4},{5,12},{6,20},{7,28},{8,32},{9,40}... | collective-permute-start | bytes 393224 | tf_op jit(solution)/shard_map/ppermute | solution.py:61
  54.3 16.0 %collective-permute-start.14 = (bf16[8,128,384]{2,1,0:T(8,128)(2,1)S(1)}, bf16[8,128,384]{2,1,0:T(8,128)(2,1)}, u32[]{:S(2)}, u32[]{:S(2)}) collective-permute-start(bf16[8,128,384]{2,1,0:T(8,128)(2,1)S(1)} %pad_maximum_fusion.1.refs_2_), channel_id=1, source_target_pairs={{0,2},{1,7},{2,0},{3,5},{4,6},{5,3},{6,4},{7,1},{64,66},{65,71},{6... | collective-permute-start | bytes 2359304 | tf_op jit(solution)/shard_map/ppermute | solution.py:83
  60.8 46.4 %all-to-all-start = ((bf16[8,32,2048]{2,1,0:T(8,128)(2,1)}), bf16[8,32,2048]{2,1,0:T(8,128)(2,1)S(1)}, u32[]{:S(2)}, u32[]{:S(2)}) async-start(bf16[8,32,2048]{2,1,0:T(8,128)(2,1)} %broadcast_in_dim.6), calls=%async_computation | async-start | bytes 2097152 | tf_op jit(solution)/shard_map/all_to_all | solution.py:109
  64.3 46.9 %collective-permute-start.15 = (bf16[8,128,512]{2,1,0:T(8,128)(2,1)S(1)}, bf16[8,128,512]{2,1,0:T(8,128)(2,1)}, u32[]{:S(2)}, u32[]{:S(2)}) collective-permute-start(bf16[8,128,512]{2,1,0:T(8,128)(2,1)S(1)} %pad_maximum_fusion.refs_0_), channel_id=1, source_target_pairs={{0,1},{1,0},{2,3},{3,2},{4,5},{5,4},{6,7},{7,6},{8,9},{9,8},{10,11... | collective-permute-start | bytes 3145736 | tf_op jit(solution)/shard_map/ppermute | solution.py:65
  70.3 40.9 %collective-permute-start.16 = (bf16[8,128,512]{2,1,0:T(8,128)(2,1)}, bf16[8,128,512]{2,1,0:T(8,128)(2,1)}, u32[]{:S(2)}, u32[]{:S(2)}) collective-permute-start(bf16[8,128,512]{2,1,0:T(8,128)(2,1)} %collective-permute-done.13.refs_1_), channel_id=1, source_target_pairs={{0,1},{1,0},{2,3},{3,2},{4,5},{5,4},{6,7},{7,6},{8,9},{9,8},{10,11... | collective-permute-start | bytes 3145736 | tf_op jit(solution)/shard_map/ppermute | solution.py:65
  71.2 25.2 %collective-permute-start.1 = (bf16[128,896]{1,0:T(8,128)(2,1)S(1)}, bf16[128,896]{1,0:T(8,128)(2,1)S(1)}, u32[]{:S(2)}, u32[]{:S(2)}) collective-permute-start(bf16[128,896]{1,0:T(8,128)(2,1)S(1)} %get-tuple-element.75), channel_id=1, source_target_pairs={{0,16},{1,48},{2,24},{3,56},{4,20},{5,52},{6,28},{7,60},{8,0},{9,3... | collective-permute-start | bytes 688136 | tf_op jit(solution)/shard_map/ppermute | solution.py:61
  75.2 36.0 %collective-permute-start.17 = (bf16[8,128,384]{2,1,0:T(8,128)(2,1)S(1)}, bf16[8,128,384]{2,1,0:T(8,128)(2,1)}, u32[]{:S(2)}, u32[]{:S(2)}) collective-permute-start(bf16[8,128,384]{2,1,0:T(8,128)(2,1)S(1)} %pad_maximum_fusion.1.refs_2_), channel_id=1, source_target_pairs={{0,1},{1,0},{2,3},{3,2},{4,5},{5,4},{6,7},{7,6},{8,9},{9,8},{10,11... | collective-permute-start | bytes 2359304 | tf_op jit(solution)/shard_map/ppermute | solution.py:65
  75.2 36.0 %collective-permute-start.18 = (bf16[8,128,384]{2,1,0:T(8,128)(2,1)}, bf16[8,128,384]{2,1,0:T(8,128)(2,1)}, u32[]{:S(2)}, u32[]{:S(2)}) collective-permute-start(bf16[8,128,384]{2,1,0:T(8,128)(2,1)} %collective-permute-done.14.refs_3_), channel_id=1, source_target_pairs={{0,1},{1,0},{2,3},{3,2},{4,5},{5,4},{6,7},{7,6},{8,9},{9,8},{10,11... | collective-permute-start | bytes 2359304 | tf_op jit(solution)/shard_map/ppermute | solution.py:65
  96.4 9.9 %collective-permute-start.2 = (bf16[128,896]{1,0:T(8,128)(2,1)}, bf16[128,896]{1,0:T(8,128)(2,1)S(1)}, u32[]{:S(2)}, u32[]{:S(2)}) collective-permute-start(bf16[128,896]{1,0:T(8,128)(2,1)} %get-tuple-element.76), channel_id=1, source_target_pairs={{0,0},{1,32},{2,8},{3,40},{4,4},{5,36},{6,12},{7,44},{8,16},{9,48}... | collective-permute-start | bytes 688136 | tf_op jit(solution)/shard_map/ppermute | solution.py:61
  128.2 12.9 %collective-permute-start.21 = (bf16[16,64,512]{2,1,0:T(8,128)(2,1)}, bf16[16,64,512]{2,1,0:T(8,128)(2,1)S(1)}, u32[]{:S(2)}, u32[]{:S(2)}) collective-permute-start(bf16[16,64,512]{2,1,0:T(8,128)(2,1)} %get-tuple-element.52), channel_id=1, source_target_pairs={{0,1},{1,0},{2,3},{3,2},{4,5},{5,4},{6,7},{7,6},{8,9},{9,8},{10,11... | collective-permute-start | bytes 3145736 | tf_op jit(solution)/shard_map/ppermute | solution.py:65
  128.2 12.9 %collective-permute-start.22 = (bf16[16,64,384]{2,1,0:T(8,128)(2,1)}, bf16[16,64,384]{2,1,0:T(8,128)(2,1)S(1)}, u32[]{:S(2)}, u32[]{:S(2)}) collective-permute-start(bf16[16,64,384]{2,1,0:T(8,128)(2,1)} %get-tuple-element.53), channel_id=1, source_target_pairs={{0,1},{1,0},{2,3},{3,2},{4,5},{5,4},{6,7},{7,6},{8,9},{9,8},{10,11... | collective-permute-start | bytes 2359304 | tf_op jit(solution)/shard_map/ppermute | solution.py:65
  132.2 8.9 %collective-permute-start.23 = (f32[2048]{0:T(1024)S(1)}, f32[2048]{0:T(1024)S(1)}, u32[]{:S(2)}, u32[]{:S(2)}) collective-permute-start(f32[2048]{0:T(1024)S(1)} %add.78), channel_id=1, source_target_pairs={{0,2},{2,0},{1,3},{3,1},{4,6},{6,4},{5,7},{7,5},{8,10},{10,8},{9,1... | collective-permute-start | bytes 24584 | tf_op jit(solution)/shard_map/ppermute | solution.py:116
  143.6 15.5 %collective-permute-start.24 = (bf16[8,64,512]{2,1,0:T(8,128)(2,1)}, bf16[8,64,512]{2,1,0:T(8,128)(2,1)}, u32[]{:S(2)}, u32[]{:S(2)}) collective-permute-start(bf16[8,64,512]{2,1,0:T(8,128)(2,1)} %slice.214), channel_id=1, source_target_pairs={{0,192},{1,65},{2,194},{3,67},{4,196},{5,69},{6,198},{7,71},{64,12... | collective-permute-start | bytes 1572872 | tf_op jit(solution)/shard_map/ppermute | solution.py:83
  145.7 13.4 %collective-permute-start.25 = (bf16[8,64,384]{2,1,0:T(8,128)(2,1)}, bf16[8,64,384]{2,1,0:T(8,128)(2,1)}, u32[]{:S(2)}, u32[]{:S(2)}) collective-permute-start(bf16[8,64,384]{2,1,0:T(8,128)(2,1)} %slice.215), channel_id=1, source_target_pairs={{0,2},{1,7},{2,0},{3,5},{4,6},{5,3},{6,4},{7,1},{64,66},{65,71},{6... | collective-permute-start | bytes 1179656 | tf_op jit(solution)/shard_map/ppermute | solution.py:83
  146.8 32.9 %all-to-all-start.1 = ((bf16[8,32,2048]{2,1,0:T(8,128)(2,1)}), bf16[8,32,2048]{2,1,0:T(8,128)(2,1)S(1)}, u32[]{:S(2)}, u32[]{:S(2)}) async-start(bf16[8,32,2048]{2,1,0:T(8,128)(2,1)} %bitcast.15), calls=%async_computation.1 | async-start | bytes 2097152 | tf_op jit(solution)/shard_map/all_to_all | solution.py:303
  160.4 9.2 %collective-permute-start.30 = (bf16[4,64,384]{2,1,0:T(8,128)(2,1)S(1)}, bf16[4,64,384]{2,1,0:T(8,128)(2,1)S(1)}, u32[]{:S(2)}, u32[]{:S(2)}) collective-permute-start(bf16[4,64,384]{2,1,0:T(8,128)(2,1)S(1)} %slice.217), channel_id=1, source_target_pairs={{0,192},{1,65},{2,194},{3,67},{4,196},{5,69},{6,198},{7,71},{64,12... | collective-permute-start | bytes 589832 | tf_op jit(solution)/shard_map/ppermute | solution.py:83
  161.9 7.8 %collective-permute-start.29 = (bf16[4,64,512]{2,1,0:T(8,128)(2,1)S(1)}, bf16[4,64,512]{2,1,0:T(8,128)(2,1)S(1)}, u32[]{:S(2)}, u32[]{:S(2)}) collective-permute-start(bf16[4,64,512]{2,1,0:T(8,128)(2,1)S(1)} %slice.216), channel_id=1, source_target_pairs={{0,6},{1,3},{2,4},{3,1},{4,2},{5,7},{6,0},{7,5},{64,70},{65,67},{6... | collective-permute-start | bytes 786440 | tf_op jit(solution)/shard_map/ppermute | solution.py:83
  169.7 10.4 %collective-permute-start.33 = (bf16[2,64,384]{2,1,0:T(8,128)(2,1)S(1)}, bf16[2,64,384]{2,1,0:T(8,128)(2,1)S(1)}, u32[]{:S(2)}, u32[]{:S(2)}) collective-permute-start(bf16[2,64,384]{2,1,0:T(8,128)(2,1)S(1)} %slice.219), channel_id=1, source_target_pairs={{0,6},{1,3},{2,4},{3,1},{4,2},{5,7},{6,0},{7,5},{64,70},{65,67},{6... | collective-permute-start | bytes 294920 | tf_op jit(solution)/shard_map/ppermute | solution.py:83
  170.4 9.7 %collective-permute-start.32 = (bf16[2,64,512]{2,1,0:T(8,128)(2,1)S(1)}, bf16[2,64,512]{2,1,0:T(8,128)(2,1)S(1)}, u32[]{:S(2)}, u32[]{:S(2)}) collective-permute-start(bf16[2,64,512]{2,1,0:T(8,128)(2,1)S(1)} %slice.218), channel_id=1, source_target_pairs={{0,64},{1,193},{2,66},{3,195},{4,68},{5,197},{6,70},{7,199},{64,0}... | collective-permute-start | bytes 393224 | tf_op jit(solution)/shard_map/ppermute | solution.py:83
  172.4 7.7 %collective-permute-start.34 = (f32[2048]{0:T(1024)S(1)}, f32[2048]{0:T(1024)S(1)}, u32[]{:S(2)}, u32[]{:S(2)}) collective-permute-start(f32[2048]{0:T(1024)S(1)} %add.87), channel_id=1, source_target_pairs={{0,8},{8,0},{1,9},{9,1},{2,10},{10,2},{3,11},{11,3},{4,12},{12,4},... | collective-permute-start | bytes 24584 | tf_op jit(solution)/shard_map/ppermute | solution.py:116
  180.2 11.2 %collective-permute-start.36 = (bf16[1,64,384]{2,1,0:T(8,128)(2,1)S(1)}, bf16[1,64,384]{2,1,0:T(8,128)(2,1)S(1)}, u32[]{:S(2)}, u32[]{:S(2)}) collective-permute-start(bf16[1,64,384]{2,1,0:T(8,128)(2,1)S(1)} %slice.221), channel_id=1, source_target_pairs={{0,64},{1,193},{2,66},{3,195},{4,68},{5,197},{6,70},{7,199},{64,0}... | collective-permute-start | bytes 147464 | tf_op jit(solution)/shard_map/ppermute | solution.py:83
  180.3 11.0 %collective-permute-start.35 = (bf16[1,64,512]{2,1,0:T(8,128)(2,1)S(1)}, bf16[1,64,512]{2,1,0:T(8,128)(2,1)S(1)}, u32[]{:S(2)}, u32[]{:S(2)}) collective-permute-start(bf16[1,64,512]{2,1,0:T(8,128)(2,1)S(1)} %slice.220), channel_id=1, source_target_pairs={{0,2},{1,7},{2,0},{3,5},{4,6},{5,3},{6,4},{7,1},{64,66},{65,71},{6... | collective-permute-start | bytes 196616 | tf_op jit(solution)/shard_map/ppermute | solution.py:83
  186.3 13.8 %collective-permute-start.19 = (bf16[32,2048]{1,0:T(8,128)(2,1)S(1)}, bf16[32,2048]{1,0:T(8,128)(2,1)S(1)}, u32[]{:S(2)}, u32[]{:S(2)}) collective-permute-start(bf16[32,2048]{1,0:T(8,128)(2,1)S(1)} %fusion.5), channel_id=1, source_target_pairs={{0,0},{8,1},{16,2},{24,3},{4,4},{12,5},{20,6},{28,7},{32,8},{40,9}... | collective-permute-start | bytes 393224 | tf_op jit(solution)/shard_map/ppermute | solution.py:61
  191.4 15.6 %collective-permute-start.39 = (bf16[32,896]{1,0:T(8,128)(2,1)S(1)}, bf16[32,896]{1,0:T(8,128)(2,1)S(1)}, u32[]{:S(2)}, u32[]{:S(2)}) collective-permute-start(bf16[32,896]{1,0:T(8,128)(2,1)S(1)} %get-tuple-element.85), channel_id=1, source_target_pairs={{16,0},{48,1},{24,2},{56,3},{0,4},{32,5},{8,6},{40,7},{17,8},{49,9... | collective-permute-start | bytes 172040 | tf_op jit(solution)/shard_map/ppermute | solution.py:61
  194.1 13.0 %collective-permute-start.40 = (bf16[32,896]{1,0:T(8,128)(2,1)S(1)}, bf16[32,896]{1,0:T(8,128)(2,1)S(1)}, u32[]{:S(2)}, u32[]{:S(2)}) collective-permute-start(bf16[32,896]{1,0:T(8,128)(2,1)S(1)} %get-tuple-element.86), channel_id=1, source_target_pairs={{0,0},{32,1},{8,2},{40,3},{16,4},{48,5},{24,6},{56,7},{1,8},{33,9}... | collective-permute-start | bytes 172040 | tf_op jit(solution)/shard_map/ppermute | solution.py:61
  (22 other events, 260.0 us)
where the time goes:
time: 211 us; the launch traced here: 208 us
  starting transfers between devices  109 us (52%)
  waiting for transfers between devices  62.2 us (29%)
  Pallas kernels  20.1 us (10%)
  other arithmetic  10.1 us (5%)
  local copies, waits for them, and re-layouts  5.74 us (3%)
    ppermute x10, starting transfers between devices, move(): return lax.ppermute(value, SWAPPED, pairs)  49.4 us
    ppermute x10, waiting for transfers between devices, move(): return lax.ppermute(value, SWAPPED, pairs)  27.8 us
    ppermute x16, starting transfers between devices, exchange(): return lax.ppermute(value, PLANE, pairs)  26.6 us
    pallas_call x3, Pallas kernels, local_call(): pl.pallas_call(kernel, out_shape=[jax.ShapeDtypeStruct(*shape) for shape...  20.1 us
    ppermute x9, waiting for transfers between devices, flip_start(): lax.ppermute(value, axes, [(i, i ^ k) for i in range(size)])  16.4 us
    ppermute x9, starting transfers between devices, flip_start(): lax.ppermute(value, axes, [(i, i ^ k) for i in range(size)])  15.7 us
    ppermute x16, waiting for transfers between devices, exchange(): return lax.ppermute(value, PLANE, pairs)  12 us
    ppermute x6, starting transfers between devices, to_peer(): return lax.ppermute(value, 'c', [(0, 1), (1, 0)])  7.13 us
  transfers between devices with their start and end apart: 43, of which 14 were waited for; matrix products, arithmetic and copies ran while one was open for 4% of the time, Pallas kernels for 2%

commit v1 on v0

--- a/solution.py
+++ b/solution.py
@@ -111,18 +111,6 @@
     )
 
 
-def flip_start(value, axes, flips):
-    size = lax.axis_size(axes)
-    return [lax.ppermute(value, axes, [(i, i ^ k) for i in range(size)]) for k in flips]
-
-
-def flip_sum(value, arrived):
-    terms = [value, *arrived]
-    while len(terms) > 1:
-        terms = [terms[k] + terms[k + 1] for k in range(0, len(terms), 2)]
-    return terms[0]
-
-
 def tile_at(tiles_ref, which, color, block):
     return tiles_ref[which * 32 + color * 16 + block]
 
@@ -139,10 +127,13 @@
         turned_ref[part, :] = normed.T
 
 
-def act_kernel(tiles_ref, core_ref, normed_ref, act_ref, rows_ref, inverse_ref, *refs):
-    sources, (gate_ref, out_ref, terms_ref) = refs[:8], refs[8:11]
-    weights, (ordered, mine, peer, total, sems) = refs[11:19], refs[19:]
+def act_kernel(
+    tiles_ref, core_ref, normed_ref, act_0_ref, act_1_ref, rows_ref, inverse_ref, *refs
+):
+    sources, (gate_ref, out_ref) = refs[:8], refs[8:10]
+    weights, (ordered, mine, peer, total, sems) = refs[10:18], refs[18:]
     core = core_ref[0] == 1
+    swapped = core_ref[1] == 1
     order = [which * 4 + color * 2 + part for color in (0, 1) for which in (0, 1) for part in (0, 1)]
     copies = {k: pltpu.make_async_copy(sources[k], weights[k], sems.at[k]) for k in order}
     for k in order:
@@ -168,7 +159,9 @@
         gate = jnp.where(core, found[1], found[0])
         up = jnp.where(core, found[0], found[1])
         sig = jax.nn.sigmoid(gate)
-        cotangent = act_ref[:, low:high].astype(F32)
+        first = act_0_ref[:, low:high].astype(F32)
+        second = act_1_ref[:, low:high].astype(F32)
+        cotangent = jnp.concatenate(in_order(first, second, swapped), axis=0)
         d_up = (cotangent * gate * sig).astype(BF16)
         d_gate = (cotangent * up * sig * (1.0 + gate * (1.0 - sig))).astype(BF16)
         gate_ref[:, low:high] = d_gate
@@ -189,12 +182,22 @@
                     tile = tile_at(tiles_ref, which, color, part * 8 + k)
                     at = pl.multiple_of(tile * 128, 128)
                     total[:, pl.ds(at, 128)] += found[:, k * 128 : (k + 1) * 128]
+    terms = []
     for k in range(16):
         part = slice(k * 128, (k + 1) * 128)
         grad = total[:, part]
         out_ref[:, part] = grad.astype(BF16)
         scaled = rows_ref[:, part].astype(F32) * inverse_ref[...]
-        terms_ref[:, part] = jnp.sum(grad * scaled, axis=0, keepdims=True)
+        terms.append(jnp.sum(grad * scaled, axis=0, keepdims=True))
+    for k in range(8):
+        found = []
+        left = terms[2 * k : 2 * k + 2]
+        for _ in range(3):
+            sent = [value.astype(BF16).astype(F32) for value in left]
+            left = [value - gone for value, gone in zip(left, sent)]
+            found.extend(sent)
+        found.append(jnp.zeros((26, 128), F32))
+        out_ref[32 * k : 32 * (k + 1), 2048:] = jnp.concatenate(found, axis=0).astype(BF16)
 
 
 def weight_grad_kernel(tiles_ref, core_ref, turned_ref, d_gate_ref, *refs):
@@ -238,7 +241,7 @@
     low = lax.axis_index("zv") == 1
     high = lax.axis_index("xh") == 1
     tiles = tiles_in_order()
-    cores = core_index.astype(jnp.int32).reshape(1)
+    cores = jnp.stack((core_index, lax.axis_index("z0"))).astype(jnp.int32)
 
     gates = in_order(w_gate[:, :HALF], w_gate[:, HALF:], high)
     ups = in_order(w_up[:, :HALF], w_up[:, HALF:], high)
@@ -279,11 +282,9 @@
         (rows, gain.reshape(1, 2048)),
         256 * 2048 * 64,
     )
-    act = jnp.concatenate(in_order(got_act[0], got_act[1], mid), axis=0)
-
-    d_gate, partial_grad, terms = local_call(
+    d_gate, partial_grad = local_call(
         act_kernel,
-        [((256, HALF), BF16), ((256, 2048), BF16), ((1, 2048), F32)],
+        [((256, HALF), BF16), ((256, 2176), BF16)],
         [
             pltpu.VMEM((8, 128, b - a), BF16)
             for a, b in (CUTS[0], CUTS[0], CUTS[1], CUTS[1]) * 2
@@ -296,14 +297,12 @@
             pltpu.SemaphoreType.DMA((8,)),
         ],
         (tiles, cores),
-        (normed, act, rows, inverse),
+        (normed, got_act[0], got_act[1], rows, inverse),
         8 * 256 * 2048 * HALF,
         weights,
     )
-    parts = lax.all_to_all(partial_grad.reshape(8, 32, 2048), Z, 0, 0, tiled=True)
-
-    terms = terms.reshape(2048)
-    terms = flip_sum(terms, flip_start(terms, "c", (1,)))
+    parts = lax.all_to_all(partial_grad.reshape(8, 32, 2176), Z, 0, 0, tiled=True)
+
     grads = local_call(
         weight_grad_kernel,
         [((16, 64, b - a), BF16) for a, b in CUTS + CUTS],
@@ -313,26 +312,24 @@
         4 * 256 * 2048 * HALF,
     )
     arrived = [to_peer(grads[2 + k]) for k in range(2)]
-    flips = flip_start(terms, "xl", (1,))
-    *arrived, flipped = lax.optimization_barrier((*arrived, *flips))
-    terms = flip_sum(terms, [flipped])
+    arrived = lax.optimization_barrier(arrived)
     summed = [grads[k].astype(F32) + arrived[k].astype(F32) for k in range(2)]
-    beside = {3: ("y", (1, 2, 3)), 2: ("xh", (1,)), 1: ("zv", (1,)), 0: ("z0", (1,))}
     for stage in (3, 2, 1, 0):
         count = 1 << stage
         going = [total.astype(BF16) for total in summed]
         arrived = [exchange(going[k][count:], k, stage) for k in range(2)]
-        flips = flip_start(terms, *beside[stage])
-        (*arrived,), (*flips,) = lax.optimization_barrier((tuple(arrived), tuple(flips)))
-        terms = flip_sum(terms, flips)
+        arrived = lax.optimization_barrier(arrived)
         summed = [summed[k][:count] + arrived[k].astype(F32) for k in range(2)]
     own_rows = jnp.concatenate([total[0].astype(BF16) for total in summed], axis=1)
     sent = in_order(own_rows[:32], own_rows[32:], mid)
     got = [move(sent[m], back(owner_pairs(m))) for m in range(2)]
     gate_weight_grad = jnp.concatenate(in_order(got[0], got[1], high), axis=1).astype(F32)
-    gain_grad = flip_sum(terms, flip_start(terms, "z1", (1,)))
-
-    own_grad = parts.astype(F32).sum(axis=0)
+
+    terms = parts[:, :6, 2048:].astype(F32).sum(axis=0).reshape(3, 256).sum(axis=0)
+    terms = sent_to_all(terms, PLANE).sum(axis=0)
+    gain_grad = sent_to_all(terms, Z).reshape(2048)
+
+    own_grad = parts[:, :, :2048].astype(F32).sum(axis=0)
     own_values = own_inputs.astype(F32)
     own_inverse = lax.rsqrt(jnp.mean(own_values * own_values, axis=-1, keepdims=True) + 1e-05)
     own_scaled = own_values * own_inverse

time: 211 us -> 195 us (0.924); the launches traced: 208 us -> 195 us
  blocking collectives: 0 us -> 25.1 us
  starting transfers between devices: 109 us -> 90.3 us
  waiting for transfers between devices: 62.2 us -> 45.8 us
  other arithmetic: 10.1 us -> 7.21 us
    all_to_all x0 -> x2, blocking collectives: none -> 25.1 us  [sent_to_all(): lax.all_to_all(jnp.broadcast_to(value[None], (peers, *value.shape)), axes...]
    ppermute x10, waiting for transfers between devices: 27.8 us -> 7.11 us  [move(): return lax.ppermute(value, SWAPPED, pairs)]
    ppermute x9 -> x0, waiting for transfers between devices: 16.4 us -> none  [flip_start(): lax.ppermute(value, axes, [(i, i ^ k) for i in range(size)])]
    ppermute x9 -> x0, starting transfers between devices: 15.7 us -> none  [flip_start(): lax.ppermute(value, axes, [(i, i ^ k) for i in range(size)])]
    ppermute x16, waiting for transfers between devices: 12 us -> 27.3 us  [exchange(): return lax.ppermute(value, PLANE, pairs)]
    ppermute x10, starting transfers between devices: 49.4 us -> 41.9 us  [move(): return lax.ppermute(value, SWAPPED, pairs)]
    all_to_all x1, starting transfers between devices: 6.8 us -> 13.1 us  [step(): lax.all_to_all(partial_grad.reshape(8, 32, 2176), Z, 0, 0, tiled=True)]
    ppermute x16, starting transfers between devices: 26.6 us -> 20.6 us  [exchange(): return lax.ppermute(value, PLANE, pairs)]
  transfers between devices with their start and end apart: 43 -> 34, of which waited for: 14 -> 13; matrix products, arithmetic and copies ran while one was open for 4% -> 3% of each run, Pallas kernels for 2% -> 2%
where the time goes in v1:
time: 195 us
  starting transfers between devices  90.3 us (46%)
  waiting for transfers between devices  45.8 us (23%)
  blocking collectives  25.1 us (13%)
  Pallas kernels  20.1 us (10%)
  other arithmetic  7.21 us (4%)
  local copies, waits for them, and re-layouts  4.99 us (3%)
    ppermute x10, starting transfers between devices, move(): return lax.ppermute(value, SWAPPED, pairs)  41.9 us
    ppermute x16, waiting for transfers between devices, exchange(): return lax.ppermute(value, PLANE, pairs)  27.3 us
    all_to_all x2, blocking collectives, sent_to_all(): lax.all_to_all(jnp.broadcast_to(value[None], (peers, *value.shape)), axes...  25.1 us
    ppermute x16, starting transfers between devices, exchange(): return lax.ppermute(value, PLANE, pairs)  20.6 us
    pallas_call x3, Pallas kernels, local_call(): pl.pallas_call(kernel, out_shape=[jax.ShapeDtypeStruct(*shape) for shape...  20.1 us
    all_to_all x1, starting transfers between devices, step(): lax.all_to_all(partial_grad.reshape(8, 32, 2176), Z, 0, 0, tiled=True)  13.1 us
    all_to_all x1, waiting for transfers between devices, step(): lax.all_to_all(partial_grad.reshape(8, 32, 2176), Z, 0, 0, tiled=True)  11.4 us
    ppermute x6, starting transfers between devices, to_peer(): return lax.ppermute(value, 'c', [(0, 1), (1, 0)])  11.1 us
  transfers between devices with their start and end apart: 34, of which 13 were waited for; matrix products, arithmetic and copies ran while one was open for 3% of the time, Pallas kernels for 2%

profile of v1, /device:TPU:1, one launch (start us, length us, event | category | flops | bytes accessed | tf_op | source)
XLA Modules:
  0.0 194.7 jit_solution(12545544260670438810)
XLA Ops:
  1.6 6.9 %collective-permute-start.3 = (bf16[32,896]{1,0:T(8,128)(2,1)S(1)}, bf16[32,896]{1,0:T(8,128)(2,1)S(1)}, u32[]{:S(2)}, u32[]{:S(2)}) collective-permute-start(bf16[32,896]{1,0:T(8,128)(2,1)S(1)} %get-tuple-element.61), channel_id=1, source_target_pairs={{0,17},{1,49},{2,25},{3,57},{4,1},{5,33},{6,9},{7,41},{8,16},{9,48... | collective-permute-start | bytes 172040 | tf_op jit(solution)/shard_map/ppermute | solution.py:61
  8.5 3.0 %collective-permute-start.4 = (bf16[32,896]{1,0:T(8,128)(2,1)S(1)}, bf16[32,896]{1,0:T(8,128)(2,1)S(1)}, u32[]{:S(2)}, u32[]{:S(2)}) collective-permute-start(bf16[32,896]{1,0:T(8,128)(2,1)S(1)} %get-tuple-element.62), channel_id=1, source_target_pairs={{0,1},{1,33},{2,9},{3,41},{4,17},{5,49},{6,25},{7,57},{8,0},{9,32}... | collective-permute-start | bytes 172040 | tf_op jit(solution)/shard_map/ppermute | solution.py:61
  11.5 3.4 %collective-permute-start.5 = (bf16[32,896]{1,0:T(8,128)(2,1)S(1)}, bf16[32,896]{1,0:T(8,128)(2,1)S(1)}, u32[]{:S(2)}, u32[]{:S(2)}) collective-permute-start(bf16[32,896]{1,0:T(8,128)(2,1)S(1)} %get-tuple-element.63), channel_id=1, source_target_pairs={{0,16},{1,48},{2,24},{3,56},{4,0},{5,32},{6,8},{7,40},{8,17},{9,49... | collective-permute-start | bytes 172040 | tf_op jit(solution)/shard_map/ppermute | solution.py:61
  14.9 4.0 %collective-permute-start.6 = (bf16[32,896]{1,0:T(8,128)(2,1)S(1)}, bf16[32,896]{1,0:T(8,128)(2,1)S(1)}, u32[]{:S(2)}, u32[]{:S(2)}) collective-permute-start(bf16[32,896]{1,0:T(8,128)(2,1)S(1)} %get-tuple-element.64), channel_id=1, source_target_pairs={{0,0},{1,32},{2,8},{3,40},{4,16},{5,48},{6,24},{7,56},{8,1},{9,33}... | collective-permute-start | bytes 172040 | tf_op jit(solution)/shard_map/ppermute | solution.py:61
  20.5 4.7 %collective-permute-start.7 = (bf16[1,128,512]{2,1,0:T(8,128)(2,1)S(1)}, bf16[1,128,512]{2,1,0:T(8,128)(2,1)S(1)}, u32[]{:S(2)}, u32[]{:S(2)}) collective-permute-start(bf16[1,128,512]{2,1,0:T(8,128)(2,1)S(1)} %fusion.8), channel_id=1, source_target_pairs={{0,2},{1,7},{2,0},{3,5},{4,6},{5,3},{6,4},{7,1},{64,66},{65,71},{6... | collective-permute-start | bytes 393224 | tf_op jit(solution)/shard_map/ppermute | solution.py:83
  25.2 2.8 %collective-permute-start.8 = (bf16[1,128,384]{2,1,0:T(8,128)(2,1)S(1)}, bf16[1,128,384]{2,1,0:T(8,128)(2,1)S(1)}, u32[]{:S(2)}, u32[]{:S(2)}) collective-permute-start(bf16[1,128,384]{2,1,0:T(8,128)(2,1)S(1)} %fusion.11), channel_id=1, source_target_pairs={{0,64},{1,193},{2,66},{3,195},{4,68},{5,197},{6,70},{7,199},{64,0}... | collective-permute-start | bytes 294920 | tf_op jit(solution)/shard_map/ppermute | solution.py:83
  28.0 2.0 %collective-permute-done.8 = bf16[1,128,384]{2,1,0:T(8,128)(2,1)S(1)} collective-permute-done((bf16[1,128,384]{2,1,0:T(8,128)(2,1)S(1)}, bf16[1,128,384]{2,1,0:T(8,128)(2,1)S(1)}, u32[]{:S(2)}, u32[]{:S(2)}) %collective-permute-start.8) | collective-permute-done | bytes 98336 | tf_op jit(solution)/shard_map/ppermute | solution.py:83
  30.1 2.8 %collective-permute-start.9 = (bf16[2,128,512]{2,1,0:T(8,128)(2,1)S(1)}, bf16[2,128,512]{2,1,0:T(8,128)(2,1)S(1)}, u32[]{:S(2)}, u32[]{:S(2)}) collective-permute-start(bf16[2,128,512]{2,1,0:T(8,128)(2,1)S(1)} %pad_maximum_fusion.4), channel_id=1, source_target_pairs={{0,64},{1,193},{2,66},{3,195},{4,68},{5,197},{6,70},{7,199},{64,0}... | collective-permute-start | bytes 786440 | tf_op jit(solution)/shard_map/ppermute | solution.py:83
  32.9 1.7 collective-permute-start.10
  34.6 3.1 %collective-permute-done.10 = bf16[2,128,384]{2,1,0:T(8,128)(2,1)S(1)} collective-permute-done((bf16[2,128,384]{2,1,0:T(8,128)(2,1)S(1)}, bf16[2,128,384]{2,1,0:T(8,128)(2,1)S(1)}, u32[]{:S(2)}, u32[]{:S(2)}) %collective-permute-start.10) | collective-permute-done | bytes 196640 | tf_op jit(solution)/shard_map/ppermute | solution.py:83
  37.7 1.5 collective-permute-start.11
  39.4 5.5 %collective-permute-start = (bf16[32,2048]{1,0:T(8,128)(2,1)S(1)}, bf16[32,2048]{1,0:T(8,128)(2,1)S(1)}, u32[]{:S(2)}, u32[]{:S(2)}) collective-permute-start(bf16[32,2048]{1,0:T(8,128)(2,1)S(1)} %copy-done.11), channel_id=1, source_target_pairs={{0,0},{1,8},{2,16},{3,24},{4,4},{5,12},{6,20},{7,28},{8,32},{9,40}... | collective-permute-start | bytes 393224 | tf_op jit(solution)/shard_map/ppermute | solution.py:61
  47.3 2.8 %collective-permute-done = bf16[32,2048]{1,0:T(8,128)(2,1)S(1)} collective-permute-done((bf16[32,2048]{1,0:T(8,128)(2,1)S(1)}, bf16[32,2048]{1,0:T(8,128)(2,1)S(1)}, u32[]{:S(2)}, u32[]{:S(2)}) %collective-permute-start) | collective-permute-done | bytes 131104 | tf_op jit(solution)/shard_map/ppermute | solution.py:61
  51.2 3.6 %all-to-all-start = ((bf16[8,32,2048]{2,1,0:T(8,128)(2,1)}), bf16[8,32,2048]{2,1,0:T(8,128)(2,1)S(1)}, u32[]{:S(2)}, u32[]{:S(2)}) async-start(bf16[8,32,2048]{2,1,0:T(8,128)(2,1)} %broadcast_in_dim.10), calls=%async_computation | async-start | bytes 2097152 | tf_op jit(solution)/shard_map/all_to_all | solution.py:109
  56.0 2.5 %collective-permute-start.14 = (bf16[8,128,384]{2,1,0:T(8,128)(2,1)S(1)}, bf16[8,128,384]{2,1,0:T(8,128)(2,1)}, u32[]{:S(2)}, u32[]{:S(2)}) collective-permute-start(bf16[8,128,384]{2,1,0:T(8,128)(2,1)S(1)} %pad_maximum_fusion.1.refs_2_), channel_id=1, source_target_pairs={{0,2},{1,7},{2,0},{3,5},{4,6},{5,3},{6,4},{7,1},{64,66},{65,71},{6... | collective-permute-start | bytes 2359304 | tf_op jit(solution)/shard_map/ppermute | solution.py:83
  58.5 3.8 %collective-permute-start.15 = (bf16[8,128,512]{2,1,0:T(8,128)(2,1)S(1)}, bf16[8,128,512]{2,1,0:T(8,128)(2,1)}, u32[]{:S(2)}, u32[]{:S(2)}) collective-permute-start(bf16[8,128,512]{2,1,0:T(8,128)(2,1)S(1)} %pad_maximum_fusion.refs_0_), channel_id=1, source_target_pairs={{0,1},{1,0},{2,3},{3,2},{4,5},{5,4},{6,7},{7,6},{8,9},{9,8},{10,11... | collective-permute-start | bytes 3145736 | tf_op jit(solution)/shard_map/ppermute | solution.py:65
  62.3 6.1 %collective-permute-done.14.refs_3_ = bf16[8,128,384]{2,1,0:T(8,128)(2,1)} collective-permute-done((bf16[8,128,384]{2,1,0:T(8,128)(2,1)S(1)}, bf16[8,128,384]{2,1,0:T(8,128)(2,1)}, u32[]{:S(2)}, u32[]{:S(2)}) %collective-permute-start.14) | collective-permute-done | bytes 786464 | tf_op jit(solution)/shard_map/ppermute | solution.py:83
  68.4 5.9 %collective-permute-start.16 = (bf16[8,128,512]{2,1,0:T(8,128)(2,1)}, bf16[8,128,512]{2,1,0:T(8,128)(2,1)}, u32[]{:S(2)}, u32[]{:S(2)}) collective-permute-start(bf16[8,128,512]{2,1,0:T(8,128)(2,1)} %collective-permute-done.13.refs_1_), channel_id=1, source_target_pairs={{0,1},{1,0},{2,3},{3,2},{4,5},{5,4},{6,7},{7,6},{8,9},{9,8},{10,11... | collective-permute-start | bytes 3145736 | tf_op jit(solution)/shard_map/ppermute | solution.py:65
  74.8 7.4 %collective-permute-start.1 = (bf16[128,896]{1,0:T(8,128)(2,1)S(1)}, bf16[128,896]{1,0:T(8,128)(2,1)S(1)}, u32[]{:S(2)}, u32[]{:S(2)}) collective-permute-start(bf16[128,896]{1,0:T(8,128)(2,1)S(1)} %get-tuple-element.58), channel_id=1, source_target_pairs={{0,0},{1,32},{2,8},{3,40},{4,4},{5,36},{6,12},{7,44},{8,16},{9,48}... | collective-permute-start | bytes 688136 | tf_op jit(solution)/shard_map/ppermute | solution.py:61
  82.3 2.9 %collective-permute-done.1.act_0_ref = bf16[128,896]{1,0:T(8,128)(2,1)S(1)} collective-permute-done((bf16[128,896]{1,0:T(8,128)(2,1)S(1)}, bf16[128,896]{1,0:T(8,128)(2,1)S(1)}, u32[]{:S(2)}, u32[]{:S(2)}) %collective-permute-start.1) | collective-permute-done | bytes 229408 | tf_op jit(solution)/shard_map/ppermute | solution.py:61
  85.2 4.3 %collective-permute-start.2 = (bf16[128,896]{1,0:T(8,128)(2,1)S(1)}, bf16[128,896]{1,0:T(8,128)(2,1)}, u32[]{:S(2)}, u32[]{:S(2)}) collective-permute-start(bf16[128,896]{1,0:T(8,128)(2,1)S(1)} %get-tuple-element.57), channel_id=1, source_target_pairs={{0,16},{1,48},{2,24},{3,56},{4,20},{5,52},{6,28},{7,60},{8,0},{9,3... | collective-permute-start | bytes 688136 | tf_op jit(solution)/shard_map/ppermute | solution.py:61
  91.6 3.2 %shard_map.94 = (bf16[256,2048]{1,0:T(8,128)(2,1)}, bf16[2048,256]{1,0:T(8,128)(2,1)}, f32[256,1]{1,0:T(8,128)}) custom-call(bf16[256,2048]{1,0:T(8,128)(2,1)} %bitcast.14, f32[1,2048]{1,0:T(1,128)} %bitcast.16), custom_call_target="tpu_custom_call" | custom-call | flops 33554432 | bytes 8388608 | tf_op jit(solution)/shard_map/pallas_call | solution.py:225
  94.9 12.7 %shard_map.95 = (bf16[256,896]{1,0:T(8,128)(2,1)}, bf16[256,2176]{1,0:T(8,128)(2,1)}) custom-call(s32[64]{0:T(128)} %fusion.15.tiles_ref, s32[2]{0:T(128)} %pad_add_fusion.core_ref, bf16[256,2048]{1,0:T(8,128)(2,1)} %get-tuple-element.30.normed_ref, bf16[128,896]{1,0:T(8,128)(2,1)} %copy-done.10, bf16[128,896]{1,0:T(8,128)(2,1)} %collective-permute-done.2.act_1_ref, ...), custom_call_target="tpu_custom_call" | custom-call | flops 3758096384 | bytes 8388608 | tf_op jit(solution)/shard_map/pallas_call | solution.py:225
  107.6 4.2 %shard_map.96 = (bf16[16,64,512]{2,1,0:T(8,128)(2,1)}, bf16[16,64,384]{2,1,0:T(8,128)(2,1)}, bf16[16,64,512]{2,1,0:T(8,128)(2,1)}, bf16[16,64,384]{2,1,0:T(8,128)(2,1)}) custom-call(s32[64]{0:T(128)} %fusion.15.tiles_ref, s32[2]{0:T(128)} %pad_add_fusion.core_ref, bf16[2048,256]{1,0:T(8,128)(2,1)} %get-tuple-element.41.turned_ref, ...), custom_call_target="tpu_custom_call" | custom-call | flops 1879048192 | bytes 8388608 | tf_op jit(solution)/shard_map/pallas_call | solution.py:225
  112.7 13.1 %all-to-all-start.1 = ((bf16[8,32,2176]{2,1,0:T(8,128)(2,1)}), bf16[8,32,2176]{2,1,0:T(8,128)(2,1)S(1)}, u32[]{:S(2)}, u32[]{:S(2)}) async-start(bf16[8,32,2176]{2,1,0:T(8,128)(2,1)} %bitcast.6), calls=%async_computation.1 | async-start | bytes 2228224 | tf_op jit(solution)/shard_map/all_to_all | solution.py:304
  129.2 8.0 %collective-permute-done.23 = bf16[8,64,384]{2,1,0:T(8,128)(2,1)S(1)} collective-permute-done((bf16[8,64,384]{2,1,0:T(8,128)(2,1)S(1)}, bf16[8,64,384]{2,1,0:T(8,128)(2,1)S(1)}, u32[]{:S(2)}, u32[]{:S(2)}) %collective-permute-start.23) | collective-permute-done | bytes 393248 | tf_op jit(solution)/shard_map/ppermute | solution.py:83
  138.2 4.3 %collective-permute-done.25 = bf16[4,64,384]{2,1,0:T(8,128)(2,1)S(1)} collective-permute-done((bf16[4,64,384]{2,1,0:T(8,128)(2,1)S(1)}, bf16[4,64,384]{2,1,0:T(8,128)(2,1)S(1)}, u32[]{:S(2)}, u32[]{:S(2)}) %collective-permute-start.25) | collective-permute-done | bytes 196640 | tf_op jit(solution)/shard_map/ppermute | solution.py:83
  145.1 11.4 %all-to-all-done.1 = bf16[8,32,2176]{2,1,0:T(8,128)(2,1)S(1)} async-done(((bf16[8,32,2176]{2,1,0:T(8,128)(2,1)}), bf16[8,32,2176]{2,1,0:T(8,128)(2,1)S(1)}, u32[]{:S(2)}, u32[]{:S(2)}) %all-to-all-start.1) | async-done | bytes 1114144 | tf_op jit(solution)/shard_map/all_to_all | solution.py:304
  158.0 2.2 %collective-permute-start.19 = (bf16[32,2048]{1,0:T(8,128)(2,1)S(1)}, bf16[32,2048]{1,0:T(8,128)(2,1)S(1)}, u32[]{:S(2)}, u32[]{:S(2)}) collective-permute-start(bf16[32,2048]{1,0:T(8,128)(2,1)S(1)} %fusion.5), channel_id=1, source_target_pairs={{0,0},{8,1},{16,2},{24,3},{4,4},{12,5},{20,6},{28,7},{32,8},{40,9}... | collective-permute-start | bytes 393224 | tf_op jit(solution)/shard_map/ppermute | solution.py:61
  162.5 5.0 %collective-permute-start.31 = (bf16[32,896]{1,0:T(8,128)(2,1)S(1)}, bf16[32,896]{1,0:T(8,128)(2,1)S(1)}, u32[]{:S(2)}, u32[]{:S(2)}) collective-permute-start(bf16[32,896]{1,0:T(8,128)(2,1)S(1)} %get-tuple-element.68), channel_id=1, source_target_pairs={{0,0},{32,1},{8,2},{40,3},{16,4},{48,5},{24,6},{56,7},{1,8},{33,9}... | collective-permute-start | bytes 172040 | tf_op jit(solution)/shard_map/ppermute | solution.py:61
  167.5 16.2 %all_to_all.22 = f32[32,1,256]{2,1,0:T(1,128)S(1)} all-to-all(f32[32,1,256]{2,1,0:T(1,128)S(1)} %broadcast_in_dim.13), channel_id=1, replica_groups=mesh['y'=4,'z1'=2,'z0'=2,'zv'=2,'xh'=2,'xl'=2,'c'=2] {'y','xh','xl','c'}, dimensions={0} | all-to-all | bytes 65536 | tf_op jit(solution)/shard_map/all_to_all | solution.py:109
  183.7 9.0 %all_to_all.23 = f32[8,1,256]{2,1,0:T(1,128)S(1)} all-to-all(f32[8,1,256]{2,1,0:T(1,128)S(1)} %broadcast_in_dim.14), channel_id=1, replica_groups=mesh['y'=4,'z1'=2,'z0'=2,'zv'=2,'xh'=2,'xl'=2,'c'=2] {'z1','z0','zv'}, dimensions={0} | all-to-all | bytes 16384 | tf_op jit(solution)/shard_map/all_to_all | solution.py:109
  (116 shorter events, 23.7 us)
Async XLA Ops:
  1.6 17.4 %collective-permute-start.3 = (bf16[32,896]{1,0:T(8,128)(2,1)S(1)}, bf16[32,896]{1,0:T(8,128)(2,1)S(1)}, u32[]{:S(2)}, u32[]{:S(2)}) collective-permute-start(bf16[32,896]{1,0:T(8,128)(2,1)S(1)} %get-tuple-element.61), channel_id=1, source_target_pairs={{0,17},{1,49},{2,25},{3,57},{4,1},{5,33},{6,9},{7,41},{8,16},{9,48... | collective-permute-start | bytes 172040 | tf_op jit(solution)/shard_map/ppermute | solution.py:61
  8.5 10.5 %collective-permute-start.4 = (bf16[32,896]{1,0:T(8,128)(2,1)S(1)}, bf16[32,896]{1,0:T(8,128)(2,1)S(1)}, u32[]{:S(2)}, u32[]{:S(2)}) collective-permute-start(bf16[32,896]{1,0:T(8,128)(2,1)S(1)} %get-tuple-element.62), channel_id=1, source_target_pairs={{0,1},{1,33},{2,9},{3,41},{4,17},{5,49},{6,25},{7,57},{8,0},{9,32}... | collective-permute-start | bytes 172040 | tf_op jit(solution)/shard_map/ppermute | solution.py:61
  11.5 7.5 %collective-permute-start.5 = (bf16[32,896]{1,0:T(8,128)(2,1)S(1)}, bf16[32,896]{1,0:T(8,128)(2,1)S(1)}, u32[]{:S(2)}, u32[]{:S(2)}) collective-permute-start(bf16[32,896]{1,0:T(8,128)(2,1)S(1)} %get-tuple-element.63), channel_id=1, source_target_pairs={{0,16},{1,48},{2,24},{3,56},{4,0},{5,32},{6,8},{7,40},{8,17},{9,49... | collective-permute-start | bytes 172040 | tf_op jit(solution)/shard_map/ppermute | solution.py:61
  14.9 5.5 %collective-permute-start.6 = (bf16[32,896]{1,0:T(8,128)(2,1)S(1)}, bf16[32,896]{1,0:T(8,128)(2,1)S(1)}, u32[]{:S(2)}, u32[]{:S(2)}) collective-permute-start(bf16[32,896]{1,0:T(8,128)(2,1)S(1)} %get-tuple-element.64), channel_id=1, source_target_pairs={{0,0},{1,32},{2,8},{3,40},{4,16},{5,48},{6,24},{7,56},{8,1},{9,33}... | collective-permute-start | bytes 172040 | tf_op jit(solution)/shard_map/ppermute | solution.py:61
  20.5 9.5 %collective-permute-start.7 = (bf16[1,128,512]{2,1,0:T(8,128)(2,1)S(1)}, bf16[1,128,512]{2,1,0:T(8,128)(2,1)S(1)}, u32[]{:S(2)}, u32[]{:S(2)}) collective-permute-start(bf16[1,128,512]{2,1,0:T(8,128)(2,1)S(1)} %fusion.8), channel_id=1, source_target_pairs={{0,2},{1,7},{2,0},{3,5},{4,6},{5,3},{6,4},{7,1},{64,66},{65,71},{6... | collective-permute-start | bytes 393224 | tf_op jit(solution)/shard_map/ppermute | solution.py:83
  25.2 4.8 %collective-permute-start.8 = (bf16[1,128,384]{2,1,0:T(8,128)(2,1)S(1)}, bf16[1,128,384]{2,1,0:T(8,128)(2,1)S(1)}, u32[]{:S(2)}, u32[]{:S(2)}) collective-permute-start(bf16[1,128,384]{2,1,0:T(8,128)(2,1)S(1)} %fusion.11), channel_id=1, source_target_pairs={{0,64},{1,193},{2,66},{3,195},{4,68},{5,197},{6,70},{7,199},{64,0}... | collective-permute-start | bytes 294920 | tf_op jit(solution)/shard_map/ppermute | solution.py:83
  30.1 7.6 %collective-permute-start.9 = (bf16[2,128,512]{2,1,0:T(8,128)(2,1)S(1)}, bf16[2,128,512]{2,1,0:T(8,128)(2,1)S(1)}, u32[]{:S(2)}, u32[]{:S(2)}) collective-permute-start(bf16[2,128,512]{2,1,0:T(8,128)(2,1)S(1)} %pad_maximum_fusion.4), channel_id=1, source_target_pairs={{0,64},{1,193},{2,66},{3,195},{4,68},{5,197},{6,70},{7,199},{64,0}... | collective-permute-start | bytes 786440 | tf_op jit(solution)/shard_map/ppermute | solution.py:83
  32.9 4.8 %collective-permute-start.10 = (bf16[2,128,384]{2,1,0:T(8,128)(2,1)S(1)}, bf16[2,128,384]{2,1,0:T(8,128)(2,1)S(1)}, u32[]{:S(2)}, u32[]{:S(2)}) collective-permute-start(bf16[2,128,384]{2,1,0:T(8,128)(2,1)S(1)} %pad_maximum_fusion.5), channel_id=1, source_target_pairs={{0,6},{1,3},{2,4},{3,1},{4,2},{5,7},{6,0},{7,5},{64,70},{65,67},{6... | collective-permute-start | bytes 589832 | tf_op jit(solution)/shard_map/ppermute | solution.py:83
  37.7 9.4 %collective-permute-start.11 = (bf16[4,128,512]{2,1,0:T(8,128)(2,1)S(1)}, bf16[4,128,512]{2,1,0:T(8,128)(2,1)S(1)}, u32[]{:S(2)}, u32[]{:S(2)}) collective-permute-start(bf16[4,128,512]{2,1,0:T(8,128)(2,1)S(1)} %pad_maximum_fusion.2), channel_id=1, source_target_pairs={{0,6},{1,3},{2,4},{3,1},{4,2},{5,7},{6,0},{7,5},{64,70},{65,67},{6... | collective-permute-start | bytes 1572872 | tf_op jit(solution)/shard_map/ppermute | solution.py:83
  39.3 7.0 %collective-permute-start.12 = (bf16[4,128,384]{2,1,0:T(8,128)(2,1)S(1)}, bf16[4,128,384]{2,1,0:T(8,128)(2,1)S(1)}, u32[]{:S(2)}, u32[]{:S(2)}) collective-permute-start(bf16[4,128,384]{2,1,0:T(8,128)(2,1)S(1)} %pad_maximum_fusion.3), channel_id=1, source_target_pairs={{0,192},{1,65},{2,194},{3,67},{4,196},{5,69},{6,198},{7,71},{64,12... | collective-permute-start | bytes 1179656 | tf_op jit(solution)/shard_map/ppermute | solution.py:83
  39.4 10.7 %collective-permute-start = (bf16[32,2048]{1,0:T(8,128)(2,1)S(1)}, bf16[32,2048]{1,0:T(8,128)(2,1)S(1)}, u32[]{:S(2)}, u32[]{:S(2)}) collective-permute-start(bf16[32,2048]{1,0:T(8,128)(2,1)S(1)} %copy-done.11), channel_id=1, source_target_pairs={{0,0},{1,8},{2,16},{3,24},{4,4},{5,12},{6,20},{7,28},{8,32},{9,40}... | collective-permute-start | bytes 393224 | tf_op jit(solution)/shard_map/ppermute | solution.py:61
  47.2 21.2 %collective-permute-start.13 = (bf16[8,128,512]{2,1,0:T(8,128)(2,1)S(1)}, bf16[8,128,512]{2,1,0:T(8,128)(2,1)}, u32[]{:S(2)}, u32[]{:S(2)}) collective-permute-start(bf16[8,128,512]{2,1,0:T(8,128)(2,1)S(1)} %pad_maximum_fusion.refs_0_), channel_id=1, source_target_pairs={{0,192},{1,65},{2,194},{3,67},{4,196},{5,69},{6,198},{7,71},{64,12... | collective-permute-start | bytes 3145736 | tf_op jit(solution)/shard_map/ppermute | solution.py:83
  51.2 39.4 %all-to-all-start = ((bf16[8,32,2048]{2,1,0:T(8,128)(2,1)}), bf16[8,32,2048]{2,1,0:T(8,128)(2,1)S(1)}, u32[]{:S(2)}, u32[]{:S(2)}) async-start(bf16[8,32,2048]{2,1,0:T(8,128)(2,1)} %broadcast_in_dim.10), calls=%async_computation | async-start | bytes 2097152 | tf_op jit(solution)/shard_map/all_to_all | solution.py:109
  56.0 12.4 %collective-permute-start.14 = (bf16[8,128,384]{2,1,0:T(8,128)(2,1)S(1)}, bf16[8,128,384]{2,1,0:T(8,128)(2,1)}, u32[]{:S(2)}, u32[]{:S(2)}) collective-permute-start(bf16[8,128,384]{2,1,0:T(8,128)(2,1)S(1)} %pad_maximum_fusion.1.refs_2_), channel_id=1, source_target_pairs={{0,2},{1,7},{2,0},{3,5},{4,6},{5,3},{6,4},{7,1},{64,66},{65,71},{6... | collective-permute-start | bytes 2359304 | tf_op jit(solution)/shard_map/ppermute | solution.py:83
  58.5 36.3 %collective-permute-start.15 = (bf16[8,128,512]{2,1,0:T(8,128)(2,1)S(1)}, bf16[8,128,512]{2,1,0:T(8,128)(2,1)}, u32[]{:S(2)}, u32[]{:S(2)}) collective-permute-start(bf16[8,128,512]{2,1,0:T(8,128)(2,1)S(1)} %pad_maximum_fusion.refs_0_), channel_id=1, source_target_pairs={{0,1},{1,0},{2,3},{3,2},{4,5},{5,4},{6,7},{7,6},{8,9},{9,8},{10,11... | collective-permute-start | bytes 3145736 | tf_op jit(solution)/shard_map/ppermute | solution.py:65
  68.4 26.4 %collective-permute-start.16 = (bf16[8,128,512]{2,1,0:T(8,128)(2,1)}, bf16[8,128,512]{2,1,0:T(8,128)(2,1)}, u32[]{:S(2)}, u32[]{:S(2)}) collective-permute-start(bf16[8,128,512]{2,1,0:T(8,128)(2,1)} %collective-permute-done.13.refs_1_), channel_id=1, source_target_pairs={{0,1},{1,0},{2,3},{3,2},{4,5},{5,4},{6,7},{7,6},{8,9},{9,8},{10,11... | collective-permute-start | bytes 3145736 | tf_op jit(solution)/shard_map/ppermute | solution.py:65
  74.2 20.6 %collective-permute-start.17 = (bf16[8,128,384]{2,1,0:T(8,128)(2,1)S(1)}, bf16[8,128,384]{2,1,0:T(8,128)(2,1)}, u32[]{:S(2)}, u32[]{:S(2)}) collective-permute-start(bf16[8,128,384]{2,1,0:T(8,128)(2,1)S(1)} %pad_maximum_fusion.1.refs_2_), channel_id=1, source_target_pairs={{0,1},{1,0},{2,3},{3,2},{4,5},{5,4},{6,7},{7,6},{8,9},{9,8},{10,11... | collective-permute-start | bytes 2359304 | tf_op jit(solution)/shard_map/ppermute | solution.py:65
  74.2 20.6 %collective-permute-start.18 = (bf16[8,128,384]{2,1,0:T(8,128)(2,1)}, bf16[8,128,384]{2,1,0:T(8,128)(2,1)}, u32[]{:S(2)}, u32[]{:S(2)}) collective-permute-start(bf16[8,128,384]{2,1,0:T(8,128)(2,1)} %collective-permute-done.14.refs_3_), channel_id=1, source_target_pairs={{0,1},{1,0},{2,3},{3,2},{4,5},{5,4},{6,7},{7,6},{8,9},{9,8},{10,11... | collective-permute-start | bytes 2359304 | tf_op jit(solution)/shard_map/ppermute | solution.py:65
  74.8 10.4 %collective-permute-start.1 = (bf16[128,896]{1,0:T(8,128)(2,1)S(1)}, bf16[128,896]{1,0:T(8,128)(2,1)S(1)}, u32[]{:S(2)}, u32[]{:S(2)}) collective-permute-start(bf16[128,896]{1,0:T(8,128)(2,1)S(1)} %get-tuple-element.58), channel_id=1, source_target_pairs={{0,0},{1,32},{2,8},{3,40},{4,4},{5,36},{6,12},{7,44},{8,16},{9,48}... | collective-permute-start | bytes 688136 | tf_op jit(solution)/shard_map/ppermute | solution.py:61
  85.2 9.6 %collective-permute-start.2 = (bf16[128,896]{1,0:T(8,128)(2,1)S(1)}, bf16[128,896]{1,0:T(8,128)(2,1)}, u32[]{:S(2)}, u32[]{:S(2)}) collective-permute-start(bf16[128,896]{1,0:T(8,128)(2,1)S(1)} %get-tuple-element.57), channel_id=1, source_target_pairs={{0,16},{1,48},{2,24},{3,56},{4,20},{5,52},{6,28},{7,60},{8,0},{9,3... | collective-permute-start | bytes 688136 | tf_op jit(solution)/shard_map/ppermute | solution.py:61
  111.8 14.1 %collective-permute-start.20 = (bf16[16,64,512]{2,1,0:T(8,128)(2,1)}, bf16[16,64,512]{2,1,0:T(8,128)(2,1)S(1)}, u32[]{:S(2)}, u32[]{:S(2)}) collective-permute-start(bf16[16,64,512]{2,1,0:T(8,128)(2,1)} %get-tuple-element.44), channel_id=1, source_target_pairs={{0,1},{1,0},{2,3},{3,2},{4,5},{5,4},{6,7},{7,6},{8,9},{9,8},{10,11... | collective-permute-start | bytes 3145736 | tf_op jit(solution)/shard_map/ppermute | solution.py:65
  112.6 13.2 %collective-permute-start.21 = (bf16[16,64,384]{2,1,0:T(8,128)(2,1)}, bf16[16,64,384]{2,1,0:T(8,128)(2,1)}, u32[]{:S(2)}, u32[]{:S(2)}) collective-permute-start(bf16[16,64,384]{2,1,0:T(8,128)(2,1)} %get-tuple-element.45), channel_id=1, source_target_pairs={{0,1},{1,0},{2,3},{3,2},{4,5},{5,4},{6,7},{7,6},{8,9},{9,8},{10,11... | collective-permute-start | bytes 2359304 | tf_op jit(solution)/shard_map/ppermute | solution.py:65
  112.7 43.7 %all-to-all-start.1 = ((bf16[8,32,2176]{2,1,0:T(8,128)(2,1)}), bf16[8,32,2176]{2,1,0:T(8,128)(2,1)S(1)}, u32[]{:S(2)}, u32[]{:S(2)}) async-start(bf16[8,32,2176]{2,1,0:T(8,128)(2,1)} %bitcast.6), calls=%async_computation.1 | async-start | bytes 2228224 | tf_op jit(solution)/shard_map/all_to_all | solution.py:304
  126.3 10.9 %collective-permute-start.22 = (bf16[8,64,512]{2,1,0:T(8,128)(2,1)S(1)}, bf16[8,64,512]{2,1,0:T(8,128)(2,1)S(1)}, u32[]{:S(2)}, u32[]{:S(2)}) collective-permute-start(bf16[8,64,512]{2,1,0:T(8,128)(2,1)S(1)} %slice.226), channel_id=1, source_target_pairs={{0,192},{1,65},{2,194},{3,67},{4,196},{5,69},{6,198},{7,71},{64,12... | collective-permute-start | bytes 1572872 | tf_op jit(solution)/shard_map/ppermute | solution.py:83
  128.7 8.4 %collective-permute-start.23 = (bf16[8,64,384]{2,1,0:T(8,128)(2,1)S(1)}, bf16[8,64,384]{2,1,0:T(8,128)(2,1)S(1)}, u32[]{:S(2)}, u32[]{:S(2)}) collective-permute-start(bf16[8,64,384]{2,1,0:T(8,128)(2,1)S(1)} %slice.227), channel_id=1, source_target_pairs={{0,2},{1,7},{2,0},{3,5},{4,6},{5,3},{6,4},{7,1},{64,66},{65,71},{6... | collective-permute-start | bytes 1179656 | tf_op jit(solution)/shard_map/ppermute | solution.py:83
  137.4 5.6 %collective-permute-start.24 = (bf16[4,64,512]{2,1,0:T(8,128)(2,1)S(1)}, bf16[4,64,512]{2,1,0:T(8,128)(2,1)S(1)}, u32[]{:S(2)}, u32[]{:S(2)}) collective-permute-start(bf16[4,64,512]{2,1,0:T(8,128)(2,1)S(1)} %slice.228), channel_id=1, source_target_pairs={{0,6},{1,3},{2,4},{3,1},{4,2},{5,7},{6,0},{7,5},{64,70},{65,67},{6... | collective-permute-start | bytes 786440 | tf_op jit(solution)/shard_map/ppermute | solution.py:83
  137.6 4.9 %collective-permute-start.25 = (bf16[4,64,384]{2,1,0:T(8,128)(2,1)S(1)}, bf16[4,64,384]{2,1,0:T(8,128)(2,1)S(1)}, u32[]{:S(2)}, u32[]{:S(2)}) collective-permute-start(bf16[4,64,384]{2,1,0:T(8,128)(2,1)S(1)} %slice.229), channel_id=1, source_target_pairs={{0,192},{1,65},{2,194},{3,67},{4,196},{5,69},{6,198},{7,71},{64,12... | collective-permute-start | bytes 589832 | tf_op jit(solution)/shard_map/ppermute | solution.py:83
  143.1 13.8 %collective-permute-start.27 = (bf16[2,64,384]{2,1,0:T(8,128)(2,1)S(1)}, bf16[2,64,384]{2,1,0:T(8,128)(2,1)S(1)}, u32[]{:S(2)}, u32[]{:S(2)}) collective-permute-start(bf16[2,64,384]{2,1,0:T(8,128)(2,1)S(1)} %slice.231), channel_id=1, source_target_pairs={{0,6},{1,3},{2,4},{3,1},{4,2},{5,7},{6,0},{7,5},{64,70},{65,67},{6... | collective-permute-start | bytes 294920 | tf_op jit(solution)/shard_map/ppermute | solution.py:83
  144.2 12.6 %collective-permute-start.26 = (bf16[2,64,512]{2,1,0:T(8,128)(2,1)S(1)}, bf16[2,64,512]{2,1,0:T(8,128)(2,1)S(1)}, u32[]{:S(2)}, u32[]{:S(2)}) collective-permute-start(bf16[2,64,512]{2,1,0:T(8,128)(2,1)S(1)} %slice.230), channel_id=1, source_target_pairs={{0,64},{1,193},{2,66},{3,195},{4,68},{5,197},{6,70},{7,199},{64,0}... | collective-permute-start | bytes 393224 | tf_op jit(solution)/shard_map/ppermute | solution.py:83
  158.0 34.7 %collective-permute-start.19 = (bf16[32,2048]{1,0:T(8,128)(2,1)S(1)}, bf16[32,2048]{1,0:T(8,128)(2,1)S(1)}, u32[]{:S(2)}, u32[]{:S(2)}) collective-permute-start(bf16[32,2048]{1,0:T(8,128)(2,1)S(1)} %fusion.5), channel_id=1, source_target_pairs={{0,0},{8,1},{16,2},{24,3},{4,4},{12,5},{20,6},{28,7},{32,8},{40,9}... | collective-permute-start | bytes 393224 | tf_op jit(solution)/shard_map/ppermute | solution.py:61
  162.3 30.4 %collective-permute-start.30 = (bf16[32,896]{1,0:T(8,128)(2,1)S(1)}, bf16[32,896]{1,0:T(8,128)(2,1)S(1)}, u32[]{:S(2)}, u32[]{:S(2)}) collective-permute-start(bf16[32,896]{1,0:T(8,128)(2,1)S(1)} %get-tuple-element.67), channel_id=1, source_target_pairs={{16,0},{48,1},{24,2},{56,3},{0,4},{32,5},{8,6},{40,7},{17,8},{49,9... | collective-permute-start | bytes 172040 | tf_op jit(solution)/shard_map/ppermute | solution.py:61
  162.5 30.3 %collective-permute-start.31 = (bf16[32,896]{1,0:T(8,128)(2,1)S(1)}, bf16[32,896]{1,0:T(8,128)(2,1)S(1)}, u32[]{:S(2)}, u32[]{:S(2)}) collective-permute-start(bf16[32,896]{1,0:T(8,128)(2,1)S(1)} %get-tuple-element.68), channel_id=1, source_target_pairs={{0,0},{32,1},{8,2},{40,3},{16,4},{48,5},{24,6},{56,7},{1,8},{33,9}... | collective-permute-start | bytes 172040 | tf_op jit(solution)/shard_map/ppermute | solution.py:61
  (14 other events, 203.3 us)

commit v2 on v1

--- a/solution.py
+++ b/solution.py
@@ -111,6 +111,15 @@
     )
 
 
+FLIPS = (("z1", 1), ("z0", 1), ("y", 1), ("y", 3), ("xh", 1), ("xl", 1), ("zv", 1), ("c", 1))
+
+
+def flipped(value, k):
+    axis, flip = FLIPS[k]
+    pairs = [(i, i ^ flip) for i in range(lax.axis_size(axis))]
+    return value + lax.ppermute(value, axis, pairs)
+
+
 def tile_at(tiles_ref, which, color, block):
     return tiles_ref[which * 32 + color * 16 + block]
 
@@ -130,8 +139,8 @@
 def act_kernel(
     tiles_ref, core_ref, normed_ref, act_0_ref, act_1_ref, rows_ref, inverse_ref, *refs
 ):
-    sources, (gate_ref, out_ref) = refs[:8], refs[8:10]
-    weights, (ordered, mine, peer, total, sems) = refs[10:18], refs[18:]
+    sources, (gate_ref, out_ref, terms_ref) = refs[:8], refs[8:11]
+    weights, (ordered, mine, peer, total, sems) = refs[11:19], refs[19:]
     core = core_ref[0] == 1
     swapped = core_ref[1] == 1
     order = [which * 4 + color * 2 + part for color in (0, 1) for which in (0, 1) for part in (0, 1)]
@@ -182,22 +191,12 @@
                     tile = tile_at(tiles_ref, which, color, part * 8 + k)
                     at = pl.multiple_of(tile * 128, 128)
                     total[:, pl.ds(at, 128)] += found[:, k * 128 : (k + 1) * 128]
-    terms = []
     for k in range(16):
         part = slice(k * 128, (k + 1) * 128)
         grad = total[:, part]
         out_ref[:, part] = grad.astype(BF16)
         scaled = rows_ref[:, part].astype(F32) * inverse_ref[...]
-        terms.append(jnp.sum(grad * scaled, axis=0, keepdims=True))
-    for k in range(8):
-        found = []
-        left = terms[2 * k : 2 * k + 2]
-        for _ in range(3):
-            sent = [value.astype(BF16).astype(F32) for value in left]
-            left = [value - gone for value, gone in zip(left, sent)]
-            found.extend(sent)
-        found.append(jnp.zeros((26, 128), F32))
-        out_ref[32 * k : 32 * (k + 1), 2048:] = jnp.concatenate(found, axis=0).astype(BF16)
+        terms_ref[:, part] = jnp.sum(grad * scaled, axis=0, keepdims=True)
 
 
 def weight_grad_kernel(tiles_ref, core_ref, turned_ref, d_gate_ref, *refs):
@@ -282,9 +281,9 @@
         (rows, gain.reshape(1, 2048)),
         256 * 2048 * 64,
     )
-    d_gate, partial_grad = local_call(
+    d_gate, partial_grad, terms = local_call(
         act_kernel,
-        [((256, HALF), BF16), ((256, 2176), BF16)],
+        [((256, HALF), BF16), ((256, 2048), BF16), ((1, 2048), F32)],
         [
             pltpu.VMEM((8, 128, b - a), BF16)
             for a, b in (CUTS[0], CUTS[0], CUTS[1], CUTS[1]) * 2
@@ -301,8 +300,9 @@
         8 * 256 * 2048 * HALF,
         weights,
     )
-    parts = lax.all_to_all(partial_grad.reshape(8, 32, 2176), Z, 0, 0, tiled=True)
-
+    parts = lax.all_to_all(partial_grad.reshape(8, 32, 2048), Z, 0, 0, tiled=True)
+
+    terms = flipped(terms.reshape(2048), 0)
     grads = local_call(
         weight_grad_kernel,
         [((16, 64, b - a), BF16) for a, b in CUTS + CUTS],
@@ -311,25 +311,29 @@
         (turned, d_gate),
         4 * 256 * 2048 * HALF,
     )
-    arrived = [to_peer(grads[2 + k]) for k in range(2)]
-    arrived = lax.optimization_barrier(arrived)
+    arrived = []
+    for color in range(2):
+        arrived.append(to_peer(grads[2 + color]))
+    *arrived, terms = lax.optimization_barrier((*arrived, flipped(terms, 1)))
     summed = [grads[k].astype(F32) + arrived[k].astype(F32) for k in range(2)]
     for stage in (3, 2, 1, 0):
         count = 1 << stage
         going = [total.astype(BF16) for total in summed]
-        arrived = [exchange(going[k][count:], k, stage) for k in range(2)]
-        arrived = lax.optimization_barrier(arrived)
+        arrived = []
+        for color in range(2):
+            arrived.append(exchange(going[color][count:], color, stage))
+        *arrived, terms = lax.optimization_barrier((*arrived, flipped(terms, 5 - stage)))
         summed = [summed[k][:count] + arrived[k].astype(F32) for k in range(2)]
     own_rows = jnp.concatenate([total[0].astype(BF16) for total in summed], axis=1)
     sent = in_order(own_rows[:32], own_rows[32:], mid)
-    got = [move(sent[m], back(owner_pairs(m))) for m in range(2)]
+    got = []
+    for m in range(2):
+        got.append(move(sent[m], back(owner_pairs(m))))
     gate_weight_grad = jnp.concatenate(in_order(got[0], got[1], high), axis=1).astype(F32)
 
-    terms = parts[:, :6, 2048:].astype(F32).sum(axis=0).reshape(3, 256).sum(axis=0)
-    terms = sent_to_all(terms, PLANE).sum(axis=0)
-    gain_grad = sent_to_all(terms, Z).reshape(2048)
-
-    own_grad = parts[:, :, :2048].astype(F32).sum(axis=0)
+    gain_grad = flipped(flipped(terms, 6), 7)
+
+    own_grad = parts.astype(F32).sum(axis=0)
     own_values = own_inputs.astype(F32)
     own_inverse = lax.rsqrt(jnp.mean(own_values * own_values, axis=-1, keepdims=True) + 1e-05)
     own_scaled = own_values * own_inverse

time: 195 us -> 189 us (0.969)
  blocking collectives: 25.1 us -> 0 us
  starting transfers between devices: 90.3 us -> 110 us
  waiting for transfers between devices: 45.8 us -> 43.7 us
    all_to_all x2 -> x0, blocking collectives: 25.1 us -> none  [sent_to_all(): lax.all_to_all(jnp.broadcast_to(value[None], (peers, *value.shape)), axes...]
    ppermute x0 -> x8, starting transfers between devices: none -> 15.6 us  [flipped(): return value + lax.ppermute(value, axis, pairs)]
    ppermute x0 -> x8, waiting for transfers between devices: none -> 11.4 us  [flipped(): return value + lax.ppermute(value, axis, pairs)]
    ppermute x16, waiting for transfers between devices: 27.3 us -> 16.9 us  [exchange(): return lax.ppermute(value, PLANE, pairs)]
    ppermute x10, starting transfers between devices: 41.9 us -> 51.8 us  [move(): return lax.ppermute(value, SWAPPED, pairs)]
    all_to_all x1, starting transfers between devices: 13.1 us -> 6.9 us  [step(): lax.all_to_all(partial_grad.reshape(8, 32, 2048), Z, 0, 0, tiled=True)]
    all_to_all x1, waiting for transfers between devices: 11.4 us -> 7.46 us  [step(): lax.all_to_all(partial_grad.reshape(8, 32, 2048), Z, 0, 0, tiled=True)]
  transfers between devices with their start and end apart: 34 -> 42, of which waited for: 13 -> 16; matrix products, arithmetic and copies ran while one was open for 3% -> 4% of each run, Pallas kernels for 2% -> 2%
where the time goes in v2:
time: 189 us; the launch traced here: 187 us
  starting transfers between devices  110 us (58%)
  waiting for transfers between devices  43.7 us (23%)
  Pallas kernels  20.1 us (11%)
  other arithmetic  8.87 us (5%)
  local copies, waits for them, and re-layouts  3.31 us (2%)
    ppermute x10, starting transfers between devices, move(): return lax.ppermute(value, SWAPPED, pairs)  51.8 us
    ppermute x16, starting transfers between devices, exchange(): return lax.ppermute(value, PLANE, pairs)  21.2 us
    pallas_call x3, Pallas kernels, local_call(): pl.pallas_call(kernel, out_shape=[jax.ShapeDtypeStruct(*shape) for shape...  20.1 us
    ppermute x16, waiting for transfers between devices, exchange(): return lax.ppermute(value, PLANE, pairs)  16.9 us
    ppermute x8, starting transfers between devices, flipped(): return value + lax.ppermute(value, axis, pairs)  15.6 us
    ppermute x8, waiting for transfers between devices, flipped(): return value + lax.ppermute(value, axis, pairs)  11.4 us
    ppermute x6, starting transfers between devices, to_peer(): return lax.ppermute(value, 'c', [(0, 1), (1, 0)])  10.6 us
    ppermute x10, waiting for transfers between devices, move(): return lax.ppermute(value, SWAPPED, pairs)  7.85 us
  transfers between devices with their start and end apart: 42, of which 16 were waited for; matrix products, arithmetic and copies ran while one was open for 4% of the time, Pallas kernels for 2%

profile of v2, /device:TPU:1, one launch (start us, length us, event | category | flops | bytes accessed | tf_op | source)
XLA Modules:
  0.0 187.0 jit_solution(14750047014633442282)
XLA Ops:
  1.6 6.9 %collective-permute-start.3 = (bf16[32,896]{1,0:T(8,128)(2,1)S(1)}, bf16[32,896]{1,0:T(8,128)(2,1)S(1)}, u32[]{:S(2)}, u32[]{:S(2)}) collective-permute-start(bf16[32,896]{1,0:T(8,128)(2,1)S(1)} %get-tuple-element.73), channel_id=1, source_target_pairs={{0,17},{1,49},{2,25},{3,57},{4,1},{5,33},{6,9},{7,41},{8,16},{9,48... | collective-permute-start | bytes 172040 | tf_op jit(solution)/shard_map/ppermute | solution.py:61
  8.5 3.0 %collective-permute-start.4 = (bf16[32,896]{1,0:T(8,128)(2,1)S(1)}, bf16[32,896]{1,0:T(8,128)(2,1)S(1)}, u32[]{:S(2)}, u32[]{:S(2)}) collective-permute-start(bf16[32,896]{1,0:T(8,128)(2,1)S(1)} %get-tuple-element.74), channel_id=1, source_target_pairs={{0,1},{1,33},{2,9},{3,41},{4,17},{5,49},{6,25},{7,57},{8,0},{9,32}... | collective-permute-start | bytes 172040 | tf_op jit(solution)/shard_map/ppermute | solution.py:61
  11.5 3.4 %collective-permute-start.5 = (bf16[32,896]{1,0:T(8,128)(2,1)S(1)}, bf16[32,896]{1,0:T(8,128)(2,1)S(1)}, u32[]{:S(2)}, u32[]{:S(2)}) collective-permute-start(bf16[32,896]{1,0:T(8,128)(2,1)S(1)} %get-tuple-element.75), channel_id=1, source_target_pairs={{0,16},{1,48},{2,24},{3,56},{4,0},{5,32},{6,8},{7,40},{8,17},{9,49... | collective-permute-start | bytes 172040 | tf_op jit(solution)/shard_map/ppermute | solution.py:61
  14.9 4.0 %collective-permute-start.6 = (bf16[32,896]{1,0:T(8,128)(2,1)S(1)}, bf16[32,896]{1,0:T(8,128)(2,1)S(1)}, u32[]{:S(2)}, u32[]{:S(2)}) collective-permute-start(bf16[32,896]{1,0:T(8,128)(2,1)S(1)} %get-tuple-element.76), channel_id=1, source_target_pairs={{0,0},{1,32},{2,8},{3,40},{4,16},{5,48},{6,24},{7,56},{8,1},{9,33}... | collective-permute-start | bytes 172040 | tf_op jit(solution)/shard_map/ppermute | solution.py:61
  20.5 4.7 %collective-permute-start.7 = (bf16[1,128,512]{2,1,0:T(8,128)(2,1)S(1)}, bf16[1,128,512]{2,1,0:T(8,128)(2,1)S(1)}, u32[]{:S(2)}, u32[]{:S(2)}) collective-permute-start(bf16[1,128,512]{2,1,0:T(8,128)(2,1)S(1)} %fusion.8), channel_id=1, source_target_pairs={{0,2},{1,7},{2,0},{3,5},{4,6},{5,3},{6,4},{7,1},{64,66},{65,71},{6... | collective-permute-start | bytes 393224 | tf_op jit(solution)/shard_map/ppermute | solution.py:83
  25.2 2.8 %collective-permute-start.8 = (bf16[1,128,384]{2,1,0:T(8,128)(2,1)S(1)}, bf16[1,128,384]{2,1,0:T(8,128)(2,1)S(1)}, u32[]{:S(2)}, u32[]{:S(2)}) collective-permute-start(bf16[1,128,384]{2,1,0:T(8,128)(2,1)S(1)} %fusion.11), channel_id=1, source_target_pairs={{0,64},{1,193},{2,66},{3,195},{4,68},{5,197},{6,70},{7,199},{64,0}... | collective-permute-start | bytes 294920 | tf_op jit(solution)/shard_map/ppermute | solution.py:83
  30.1 2.8 %collective-permute-start.9 = (bf16[2,128,512]{2,1,0:T(8,128)(2,1)S(1)}, bf16[2,128,512]{2,1,0:T(8,128)(2,1)S(1)}, u32[]{:S(2)}, u32[]{:S(2)}) collective-permute-start(bf16[2,128,512]{2,1,0:T(8,128)(2,1)S(1)} %pad_maximum_fusion.4), channel_id=1, source_target_pairs={{0,64},{1,193},{2,66},{3,195},{4,68},{5,197},{6,70},{7,199},{64,0}... | collective-permute-start | bytes 786440 | tf_op jit(solution)/shard_map/ppermute | solution.py:83
  34.6 3.1 %collective-permute-done.10 = bf16[2,128,384]{2,1,0:T(8,128)(2,1)S(1)} collective-permute-done((bf16[2,128,384]{2,1,0:T(8,128)(2,1)S(1)}, bf16[2,128,384]{2,1,0:T(8,128)(2,1)S(1)}, u32[]{:S(2)}, u32[]{:S(2)}) %collective-permute-start.10) | collective-permute-done | bytes 196640 | tf_op jit(solution)/shard_map/ppermute | solution.py:83
  39.4 5.5 %collective-permute-start = (bf16[32,2048]{1,0:T(8,128)(2,1)S(1)}, bf16[32,2048]{1,0:T(8,128)(2,1)S(1)}, u32[]{:S(2)}, u32[]{:S(2)}) collective-permute-start(bf16[32,2048]{1,0:T(8,128)(2,1)S(1)} %copy-done.11), channel_id=1, source_target_pairs={{0,0},{1,8},{2,16},{3,24},{4,4},{5,12},{6,20},{7,28},{8,32},{9,40}... | collective-permute-start | bytes 393224 | tf_op jit(solution)/shard_map/ppermute | solution.py:61
  46.6 3.5 %collective-permute-done = bf16[32,2048]{1,0:T(8,128)(2,1)S(1)} collective-permute-done((bf16[32,2048]{1,0:T(8,128)(2,1)S(1)}, bf16[32,2048]{1,0:T(8,128)(2,1)S(1)}, u32[]{:S(2)}, u32[]{:S(2)}) %collective-permute-start) | collective-permute-done | bytes 131104 | tf_op jit(solution)/shard_map/ppermute | solution.py:61
  51.2 3.7 %all-to-all-start = ((bf16[8,32,2048]{2,1,0:T(8,128)(2,1)}), bf16[8,32,2048]{2,1,0:T(8,128)(2,1)S(1)}, u32[]{:S(2)}, u32[]{:S(2)}) async-start(bf16[8,32,2048]{2,1,0:T(8,128)(2,1)} %broadcast_in_dim.6), calls=%async_computation | async-start | bytes 2097152 | tf_op jit(solution)/shard_map/all_to_all | solution.py:109
  56.0 2.5 %collective-permute-start.14 = (bf16[8,128,384]{2,1,0:T(8,128)(2,1)S(1)}, bf16[8,128,384]{2,1,0:T(8,128)(2,1)}, u32[]{:S(2)}, u32[]{:S(2)}) collective-permute-start(bf16[8,128,384]{2,1,0:T(8,128)(2,1)S(1)} %pad_maximum_fusion.1.refs_2_), channel_id=1, source_target_pairs={{0,2},{1,7},{2,0},{3,5},{4,6},{5,3},{6,4},{7,1},{64,66},{65,71},{6... | collective-permute-start | bytes 2359304 | tf_op jit(solution)/shard_map/ppermute | solution.py:83
  58.6 3.8 %collective-permute-start.15 = (bf16[8,128,512]{2,1,0:T(8,128)(2,1)S(1)}, bf16[8,128,512]{2,1,0:T(8,128)(2,1)}, u32[]{:S(2)}, u32[]{:S(2)}) collective-permute-start(bf16[8,128,512]{2,1,0:T(8,128)(2,1)S(1)} %pad_maximum_fusion.refs_0_), channel_id=1, source_target_pairs={{0,1},{1,0},{2,3},{3,2},{4,5},{5,4},{6,7},{7,6},{8,9},{9,8},{10,11... | collective-permute-start | bytes 3145736 | tf_op jit(solution)/shard_map/ppermute | solution.py:65
  62.3 6.1 %collective-permute-done.14.refs_3_ = bf16[8,128,384]{2,1,0:T(8,128)(2,1)} collective-permute-done((bf16[8,128,384]{2,1,0:T(8,128)(2,1)S(1)}, bf16[8,128,384]{2,1,0:T(8,128)(2,1)}, u32[]{:S(2)}, u32[]{:S(2)}) %collective-permute-start.14) | collective-permute-done | bytes 786464 | tf_op jit(solution)/shard_map/ppermute | solution.py:83
  68.5 5.9 %collective-permute-start.16 = (bf16[8,128,512]{2,1,0:T(8,128)(2,1)}, bf16[8,128,512]{2,1,0:T(8,128)(2,1)}, u32[]{:S(2)}, u32[]{:S(2)}) collective-permute-start(bf16[8,128,512]{2,1,0:T(8,128)(2,1)} %collective-permute-done.13.refs_1_), channel_id=1, source_target_pairs={{0,1},{1,0},{2,3},{3,2},{4,5},{5,4},{6,7},{7,6},{8,9},{9,8},{10,11... | collective-permute-start | bytes 3145736 | tf_op jit(solution)/shard_map/ppermute | solution.py:65
  75.9 7.4 %collective-permute-start.1 = (bf16[128,896]{1,0:T(8,128)(2,1)S(1)}, bf16[128,896]{1,0:T(8,128)(2,1)S(1)}, u32[]{:S(2)}, u32[]{:S(2)}) collective-permute-start(bf16[128,896]{1,0:T(8,128)(2,1)S(1)} %get-tuple-element.70), channel_id=1, source_target_pairs={{0,0},{1,32},{2,8},{3,40},{4,4},{5,36},{6,12},{7,44},{8,16},{9,48}... | collective-permute-start | bytes 688136 | tf_op jit(solution)/shard_map/ppermute | solution.py:61
  83.4 2.9 %collective-permute-done.1.act_0_ref = bf16[128,896]{1,0:T(8,128)(2,1)S(1)} collective-permute-done((bf16[128,896]{1,0:T(8,128)(2,1)S(1)}, bf16[128,896]{1,0:T(8,128)(2,1)S(1)}, u32[]{:S(2)}, u32[]{:S(2)}) %collective-permute-start.1) | collective-permute-done | bytes 229408 | tf_op jit(solution)/shard_map/ppermute | solution.py:61
  86.3 5.2 %collective-permute-start.2 = (bf16[128,896]{1,0:T(8,128)(2,1)S(1)}, bf16[128,896]{1,0:T(8,128)(2,1)}, u32[]{:S(2)}, u32[]{:S(2)}) collective-permute-start(bf16[128,896]{1,0:T(8,128)(2,1)S(1)} %get-tuple-element.69), channel_id=1, source_target_pairs={{0,16},{1,48},{2,24},{3,56},{4,20},{5,52},{6,28},{7,60},{8,0},{9,3... | collective-permute-start | bytes 688136 | tf_op jit(solution)/shard_map/ppermute | solution.py:61
  93.8 3.2 %shard_map.94 = (bf16[256,2048]{1,0:T(8,128)(2,1)}, bf16[2048,256]{1,0:T(8,128)(2,1)}, f32[256,1]{1,0:T(8,128)}) custom-call(bf16[256,2048]{1,0:T(8,128)(2,1)} %bitcast.14, f32[1,2048]{1,0:T(1,128)} %bitcast.16), custom_call_target="tpu_custom_call" | custom-call | flops 33554432 | bytes 8388608 | tf_op jit(solution)/shard_map/pallas_call | solution.py:224
  97.0 12.7 %shard_map.95 = (bf16[256,896]{1,0:T(8,128)(2,1)}, bf16[256,2048]{1,0:T(8,128)(2,1)}, f32[1,2048]{1,0:T(1,128)}) custom-call(s32[64]{0:T(128)} %fusion.15.tiles_ref, s32[2]{0:T(128)} %pad_add_fusion.core_ref, bf16[256,2048]{1,0:T(8,128)(2,1)} %get-tuple-element.36.normed_ref, bf16[128,896]{1,0:T(8,128)(2,1)} %copy-done.10, ...), custom_call_target="tpu_custom_call" | custom-call | flops 3758096384 | bytes 8388608 | tf_op jit(solution)/shard_map/pallas_call | solution.py:224
  109.7 4.2 %shard_map.96 = (bf16[16,64,512]{2,1,0:T(8,128)(2,1)}, bf16[16,64,384]{2,1,0:T(8,128)(2,1)}, bf16[16,64,512]{2,1,0:T(8,128)(2,1)}, bf16[16,64,384]{2,1,0:T(8,128)(2,1)}) custom-call(s32[64]{0:T(128)} %fusion.15.tiles_ref, s32[2]{0:T(128)} %pad_add_fusion.core_ref, bf16[2048,256]{1,0:T(8,128)(2,1)} %get-tuple-element.47.turned_ref, ...), custom_call_target="tpu_custom_call" | custom-call | flops 1879048192 | bytes 8388608 | tf_op jit(solution)/shard_map/pallas_call | solution.py:224
  114.5 7.2 %collective-permute-start.22 = (f32[2048]{0:T(1024)S(1)}, f32[2048]{0:T(1024)S(1)}, u32[]{:S(2)}, u32[]{:S(2)}) collective-permute-start(f32[2048]{0:T(1024)S(1)} %bitcast.17), channel_id=1, source_target_pairs={{0,32},{32,0},{1,33},{33,1},{2,34},{34,2},{3,35},{35,3},{4,36},{36... | collective-permute-start | bytes 24584 | tf_op jit(solution)/shard_map/ppermute | solution.py:120
  122.7 3.2 %collective-permute-start.23 = (f32[2048]{0:T(1024)S(1)}, f32[2048]{0:T(1024)S(1)}, u32[]{:S(2)}, u32[]{:S(2)}) collective-permute-start(f32[2048]{0:T(1024)S(1)} %add.75), channel_id=1, source_target_pairs={{0,16},{16,0},{1,17},{17,1},{2,18},{18,2},{3,19},{19,3},{4,20},{20... | collective-permute-start | bytes 24584 | tf_op jit(solution)/shard_map/ppermute | solution.py:120
  125.9 6.9 %all-to-all-start.1 = ((bf16[8,32,2048]{2,1,0:T(8,128)(2,1)}), bf16[8,32,2048]{2,1,0:T(8,128)(2,1)S(1)}, u32[]{:S(2)}, u32[]{:S(2)}) async-start(bf16[8,32,2048]{2,1,0:T(8,128)(2,1)} %bitcast.6), calls=%async_computation.1 | async-start | bytes 2097152 | tf_op jit(solution)/shard_map/all_to_all | solution.py:303
  137.5 4.2 %collective-permute-done.26 = f32[2048]{0:T(1024)S(1)} collective-permute-done((f32[2048]{0:T(1024)S(1)}, f32[2048]{0:T(1024)S(1)}, u32[]{:S(2)}, u32[]{:S(2)}) %collective-permute-start.26) | collective-permute-done | bytes 8224 | tf_op jit(solution)/shard_map/ppermute | solution.py:120
  145.1 2.5 %collective-permute-done.29 = f32[2048]{0:T(1024)S(1)} collective-permute-done((f32[2048]{0:T(1024)S(1)}, f32[2048]{0:T(1024)S(1)}, u32[]{:S(2)}, u32[]{:S(2)}) %collective-permute-start.29) | collective-permute-done | bytes 8224 | tf_op jit(solution)/shard_map/ppermute | solution.py:120
  150.1 2.5 %collective-permute-start.32 = (f32[2048]{0:T(1024)S(1)}, f32[2048]{0:T(1024)S(1)}, u32[]{:S(2)}, u32[]{:S(2)}) collective-permute-start(f32[2048]{0:T(1024)S(1)} %add.82), channel_id=1, source_target_pairs={{0,4},{4,0},{1,5},{5,1},{2,6},{6,2},{3,7},{7,3},{8,12},{12,8},{9,1... | collective-permute-start | bytes 24584 | tf_op jit(solution)/shard_map/ppermute | solution.py:120
  154.5 7.5 %all-to-all-done.1 = bf16[8,32,2048]{2,1,0:T(8,128)(2,1)S(1)} async-done(((bf16[8,32,2048]{2,1,0:T(8,128)(2,1)}), bf16[8,32,2048]{2,1,0:T(8,128)(2,1)S(1)}, u32[]{:S(2)}, u32[]{:S(2)}) %all-to-all-start.1) | async-done | bytes 1048608 | tf_op jit(solution)/shard_map/all_to_all | solution.py:303
  164.4 6.9 %collective-permute-start.19 = (bf16[32,2048]{1,0:T(8,128)(2,1)S(1)}, bf16[32,2048]{1,0:T(8,128)(2,1)S(1)}, u32[]{:S(2)}, u32[]{:S(2)}) collective-permute-start(bf16[32,2048]{1,0:T(8,128)(2,1)S(1)} %fusion.5), channel_id=1, source_target_pairs={{0,0},{8,1},{16,2},{24,3},{4,4},{12,5},{20,6},{28,7},{32,8},{40,9}... | collective-permute-start | bytes 393224 | tf_op jit(solution)/shard_map/ppermute | solution.py:61
  171.4 2.8 %collective-permute-start.38 = (bf16[32,896]{1,0:T(8,128)(2,1)S(1)}, bf16[32,896]{1,0:T(8,128)(2,1)S(1)}, u32[]{:S(2)}, u32[]{:S(2)}) collective-permute-start(bf16[32,896]{1,0:T(8,128)(2,1)S(1)} %get-tuple-element.79), channel_id=1, source_target_pairs={{16,0},{48,1},{24,2},{56,3},{0,4},{32,5},{8,6},{40,7},{17,8},{49,9... | collective-permute-start | bytes 172040 | tf_op jit(solution)/shard_map/ppermute | solution.py:61
  174.2 6.5 %collective-permute-start.39 = (bf16[32,896]{1,0:T(8,128)(2,1)S(1)}, bf16[32,896]{1,0:T(8,128)(2,1)S(1)}, u32[]{:S(2)}, u32[]{:S(2)}) collective-permute-start(bf16[32,896]{1,0:T(8,128)(2,1)S(1)} %get-tuple-element.80), channel_id=1, source_target_pairs={{0,0},{32,1},{8,2},{40,3},{16,4},{48,5},{24,6},{56,7},{1,8},{33,9}... | collective-permute-start | bytes 172040 | tf_op jit(solution)/shard_map/ppermute | solution.py:61
  180.8 2.9 %collective-permute-done.36 = f32[2048]{0:T(1024)S(1)} collective-permute-done((f32[2048]{0:T(1024)S(1)}, f32[2048]{0:T(1024)S(1)}, u32[]{:S(2)}, u32[]{:S(2)}) %collective-permute-start.36) | collective-permute-done | bytes 8224 | tf_op jit(solution)/shard_map/ppermute | solution.py:120
  (131 shorter events, 35.3 us)
Async XLA Ops:
  1.6 17.4 %collective-permute-start.3 = (bf16[32,896]{1,0:T(8,128)(2,1)S(1)}, bf16[32,896]{1,0:T(8,128)(2,1)S(1)}, u32[]{:S(2)}, u32[]{:S(2)}) collective-permute-start(bf16[32,896]{1,0:T(8,128)(2,1)S(1)} %get-tuple-element.73), channel_id=1, source_target_pairs={{0,17},{1,49},{2,25},{3,57},{4,1},{5,33},{6,9},{7,41},{8,16},{9,48... | collective-permute-start | bytes 172040 | tf_op jit(solution)/shard_map/ppermute | solution.py:61
  8.5 10.5 %collective-permute-start.4 = (bf16[32,896]{1,0:T(8,128)(2,1)S(1)}, bf16[32,896]{1,0:T(8,128)(2,1)S(1)}, u32[]{:S(2)}, u32[]{:S(2)}) collective-permute-start(bf16[32,896]{1,0:T(8,128)(2,1)S(1)} %get-tuple-element.74), channel_id=1, source_target_pairs={{0,1},{1,33},{2,9},{3,41},{4,17},{5,49},{6,25},{7,57},{8,0},{9,32}... | collective-permute-start | bytes 172040 | tf_op jit(solution)/shard_map/ppermute | solution.py:61
  11.5 7.5 %collective-permute-start.5 = (bf16[32,896]{1,0:T(8,128)(2,1)S(1)}, bf16[32,896]{1,0:T(8,128)(2,1)S(1)}, u32[]{:S(2)}, u32[]{:S(2)}) collective-permute-start(bf16[32,896]{1,0:T(8,128)(2,1)S(1)} %get-tuple-element.75), channel_id=1, source_target_pairs={{0,16},{1,48},{2,24},{3,56},{4,0},{5,32},{6,8},{7,40},{8,17},{9,49... | collective-permute-start | bytes 172040 | tf_op jit(solution)/shard_map/ppermute | solution.py:61
  20.5 9.5 %collective-permute-start.7 = (bf16[1,128,512]{2,1,0:T(8,128)(2,1)S(1)}, bf16[1,128,512]{2,1,0:T(8,128)(2,1)S(1)}, u32[]{:S(2)}, u32[]{:S(2)}) collective-permute-start(bf16[1,128,512]{2,1,0:T(8,128)(2,1)S(1)} %fusion.8), channel_id=1, source_target_pairs={{0,2},{1,7},{2,0},{3,5},{4,6},{5,3},{6,4},{7,1},{64,66},{65,71},{6... | collective-permute-start | bytes 393224 | tf_op jit(solution)/shard_map/ppermute | solution.py:83
  30.1 7.6 %collective-permute-start.9 = (bf16[2,128,512]{2,1,0:T(8,128)(2,1)S(1)}, bf16[2,128,512]{2,1,0:T(8,128)(2,1)S(1)}, u32[]{:S(2)}, u32[]{:S(2)}) collective-permute-start(bf16[2,128,512]{2,1,0:T(8,128)(2,1)S(1)} %pad_maximum_fusion.4), channel_id=1, source_target_pairs={{0,64},{1,193},{2,66},{3,195},{4,68},{5,197},{6,70},{7,199},{64,0}... | collective-permute-start | bytes 786440 | tf_op jit(solution)/shard_map/ppermute | solution.py:83
  37.7 8.6 %collective-permute-start.11 = (bf16[4,128,512]{2,1,0:T(8,128)(2,1)S(1)}, bf16[4,128,512]{2,1,0:T(8,128)(2,1)S(1)}, u32[]{:S(2)}, u32[]{:S(2)}) collective-permute-start(bf16[4,128,512]{2,1,0:T(8,128)(2,1)S(1)} %pad_maximum_fusion.2), channel_id=1, source_target_pairs={{0,6},{1,3},{2,4},{3,1},{4,2},{5,7},{6,0},{7,5},{64,70},{65,67},{6... | collective-permute-start | bytes 1572872 | tf_op jit(solution)/shard_map/ppermute | solution.py:83
  39.4 10.7 %collective-permute-start = (bf16[32,2048]{1,0:T(8,128)(2,1)S(1)}, bf16[32,2048]{1,0:T(8,128)(2,1)S(1)}, u32[]{:S(2)}, u32[]{:S(2)}) collective-permute-start(bf16[32,2048]{1,0:T(8,128)(2,1)S(1)} %copy-done.11), channel_id=1, source_target_pairs={{0,0},{1,8},{2,16},{3,24},{4,4},{5,12},{6,20},{7,28},{8,32},{9,40}... | collective-permute-start | bytes 393224 | tf_op jit(solution)/shard_map/ppermute | solution.py:61
  46.5 22.0 %collective-permute-start.13 = (bf16[8,128,512]{2,1,0:T(8,128)(2,1)S(1)}, bf16[8,128,512]{2,1,0:T(8,128)(2,1)}, u32[]{:S(2)}, u32[]{:S(2)}) collective-permute-start(bf16[8,128,512]{2,1,0:T(8,128)(2,1)S(1)} %pad_maximum_fusion.refs_0_), channel_id=1, source_target_pairs={{0,192},{1,65},{2,194},{3,67},{4,196},{5,69},{6,198},{7,71},{64,12... | collective-permute-start | bytes 3145736 | tf_op jit(solution)/shard_map/ppermute | solution.py:83
  51.2 41.6 %all-to-all-start = ((bf16[8,32,2048]{2,1,0:T(8,128)(2,1)}), bf16[8,32,2048]{2,1,0:T(8,128)(2,1)S(1)}, u32[]{:S(2)}, u32[]{:S(2)}) async-start(bf16[8,32,2048]{2,1,0:T(8,128)(2,1)} %broadcast_in_dim.6), calls=%async_computation | async-start | bytes 2097152 | tf_op jit(solution)/shard_map/all_to_all | solution.py:109
  56.0 12.4 %collective-permute-start.14 = (bf16[8,128,384]{2,1,0:T(8,128)(2,1)S(1)}, bf16[8,128,384]{2,1,0:T(8,128)(2,1)}, u32[]{:S(2)}, u32[]{:S(2)}) collective-permute-start(bf16[8,128,384]{2,1,0:T(8,128)(2,1)S(1)} %pad_maximum_fusion.1.refs_2_), channel_id=1, source_target_pairs={{0,2},{1,7},{2,0},{3,5},{4,6},{5,3},{6,4},{7,1},{64,66},{65,71},{6... | collective-permute-start | bytes 2359304 | tf_op jit(solution)/shard_map/ppermute | solution.py:83
  58.6 38.4 %collective-permute-start.15 = (bf16[8,128,512]{2,1,0:T(8,128)(2,1)S(1)}, bf16[8,128,512]{2,1,0:T(8,128)(2,1)}, u32[]{:S(2)}, u32[]{:S(2)}) collective-permute-start(bf16[8,128,512]{2,1,0:T(8,128)(2,1)S(1)} %pad_maximum_fusion.refs_0_), channel_id=1, source_target_pairs={{0,1},{1,0},{2,3},{3,2},{4,5},{5,4},{6,7},{7,6},{8,9},{9,8},{10,11... | collective-permute-start | bytes 3145736 | tf_op jit(solution)/shard_map/ppermute | solution.py:65
  68.5 28.5 %collective-permute-start.16 = (bf16[8,128,512]{2,1,0:T(8,128)(2,1)}, bf16[8,128,512]{2,1,0:T(8,128)(2,1)}, u32[]{:S(2)}, u32[]{:S(2)}) collective-permute-start(bf16[8,128,512]{2,1,0:T(8,128)(2,1)} %collective-permute-done.13.refs_1_), channel_id=1, source_target_pairs={{0,1},{1,0},{2,3},{3,2},{4,5},{5,4},{6,7},{7,6},{8,9},{9,8},{10,11... | collective-permute-start | bytes 3145736 | tf_op jit(solution)/shard_map/ppermute | solution.py:65
  74.3 22.6 %collective-permute-start.17 = (bf16[8,128,384]{2,1,0:T(8,128)(2,1)S(1)}, bf16[8,128,384]{2,1,0:T(8,128)(2,1)}, u32[]{:S(2)}, u32[]{:S(2)}) collective-permute-start(bf16[8,128,384]{2,1,0:T(8,128)(2,1)S(1)} %pad_maximum_fusion.1.refs_2_), channel_id=1, source_target_pairs={{0,1},{1,0},{2,3},{3,2},{4,5},{5,4},{6,7},{7,6},{8,9},{9,8},{10,11... | collective-permute-start | bytes 2359304 | tf_op jit(solution)/shard_map/ppermute | solution.py:65
  74.3 22.6 %collective-permute-start.18 = (bf16[8,128,384]{2,1,0:T(8,128)(2,1)}, bf16[8,128,384]{2,1,0:T(8,128)(2,1)}, u32[]{:S(2)}, u32[]{:S(2)}) collective-permute-start(bf16[8,128,384]{2,1,0:T(8,128)(2,1)} %collective-permute-done.14.refs_3_), channel_id=1, source_target_pairs={{0,1},{1,0},{2,3},{3,2},{4,5},{5,4},{6,7},{7,6},{8,9},{9,8},{10,11... | collective-permute-start | bytes 2359304 | tf_op jit(solution)/shard_map/ppermute | solution.py:65
  75.9 10.4 %collective-permute-start.1 = (bf16[128,896]{1,0:T(8,128)(2,1)S(1)}, bf16[128,896]{1,0:T(8,128)(2,1)S(1)}, u32[]{:S(2)}, u32[]{:S(2)}) collective-permute-start(bf16[128,896]{1,0:T(8,128)(2,1)S(1)} %get-tuple-element.70), channel_id=1, source_target_pairs={{0,0},{1,32},{2,8},{3,40},{4,4},{5,36},{6,12},{7,44},{8,16},{9,48}... | collective-permute-start | bytes 688136 | tf_op jit(solution)/shard_map/ppermute | solution.py:61
  86.3 10.6 %collective-permute-start.2 = (bf16[128,896]{1,0:T(8,128)(2,1)S(1)}, bf16[128,896]{1,0:T(8,128)(2,1)}, u32[]{:S(2)}, u32[]{:S(2)}) collective-permute-start(bf16[128,896]{1,0:T(8,128)(2,1)S(1)} %get-tuple-element.69), channel_id=1, source_target_pairs={{0,16},{1,48},{2,24},{3,56},{4,20},{5,52},{6,28},{7,60},{8,0},{9,3... | collective-permute-start | bytes 688136 | tf_op jit(solution)/shard_map/ppermute | solution.py:61
  114.0 18.8 %collective-permute-start.20 = (bf16[16,64,512]{2,1,0:T(8,128)(2,1)}, bf16[16,64,512]{2,1,0:T(8,128)(2,1)S(1)}, u32[]{:S(2)}, u32[]{:S(2)}) collective-permute-start(bf16[16,64,512]{2,1,0:T(8,128)(2,1)} %get-tuple-element.50), channel_id=1, source_target_pairs={{0,1},{1,0},{2,3},{3,2},{4,5},{5,4},{6,7},{7,6},{8,9},{9,8},{10,11... | collective-permute-start | bytes 3145736 | tf_op jit(solution)/shard_map/ppermute | solution.py:65
  114.0 18.8 %collective-permute-start.21 = (bf16[16,64,384]{2,1,0:T(8,128)(2,1)}, bf16[16,64,384]{2,1,0:T(8,128)(2,1)}, u32[]{:S(2)}, u32[]{:S(2)}) collective-permute-start(bf16[16,64,384]{2,1,0:T(8,128)(2,1)} %get-tuple-element.51), channel_id=1, source_target_pairs={{0,1},{1,0},{2,3},{3,2},{4,5},{5,4},{6,7},{7,6},{8,9},{9,8},{10,11... | collective-permute-start | bytes 2359304 | tf_op jit(solution)/shard_map/ppermute | solution.py:65
  114.5 8.2 %collective-permute-start.22 = (f32[2048]{0:T(1024)S(1)}, f32[2048]{0:T(1024)S(1)}, u32[]{:S(2)}, u32[]{:S(2)}) collective-permute-start(f32[2048]{0:T(1024)S(1)} %bitcast.17), channel_id=1, source_target_pairs={{0,32},{32,0},{1,33},{33,1},{2,34},{34,2},{3,35},{35,3},{4,36},{36... | collective-permute-start | bytes 24584 | tf_op jit(solution)/shard_map/ppermute | solution.py:120
  122.7 10.1 %collective-permute-start.23 = (f32[2048]{0:T(1024)S(1)}, f32[2048]{0:T(1024)S(1)}, u32[]{:S(2)}, u32[]{:S(2)}) collective-permute-start(f32[2048]{0:T(1024)S(1)} %add.75), channel_id=1, source_target_pairs={{0,16},{16,0},{1,17},{17,1},{2,18},{18,2},{3,19},{19,3},{4,20},{20... | collective-permute-start | bytes 24584 | tf_op jit(solution)/shard_map/ppermute | solution.py:120
  125.9 36.1 %all-to-all-start.1 = ((bf16[8,32,2048]{2,1,0:T(8,128)(2,1)}), bf16[8,32,2048]{2,1,0:T(8,128)(2,1)S(1)}, u32[]{:S(2)}, u32[]{:S(2)}) async-start(bf16[8,32,2048]{2,1,0:T(8,128)(2,1)} %bitcast.6), calls=%async_computation.1 | async-start | bytes 2097152 | tf_op jit(solution)/shard_map/all_to_all | solution.py:303
  133.3 10.3 %collective-permute-start.24 = (bf16[8,64,512]{2,1,0:T(8,128)(2,1)S(1)}, bf16[8,64,512]{2,1,0:T(8,128)(2,1)S(1)}, u32[]{:S(2)}, u32[]{:S(2)}) collective-permute-start(bf16[8,64,512]{2,1,0:T(8,128)(2,1)S(1)} %slice.214), channel_id=1, source_target_pairs={{0,192},{1,65},{2,194},{3,67},{4,196},{5,69},{6,198},{7,71},{64,12... | collective-permute-start | bytes 1572872 | tf_op jit(solution)/shard_map/ppermute | solution.py:83
  135.3 8.2 %collective-permute-start.25 = (bf16[8,64,384]{2,1,0:T(8,128)(2,1)S(1)}, bf16[8,64,384]{2,1,0:T(8,128)(2,1)S(1)}, u32[]{:S(2)}, u32[]{:S(2)}) collective-permute-start(bf16[8,64,384]{2,1,0:T(8,128)(2,1)S(1)} %slice.215), channel_id=1, source_target_pairs={{0,2},{1,7},{2,0},{3,5},{4,6},{5,3},{6,4},{7,1},{64,66},{65,71},{6... | collective-permute-start | bytes 1179656 | tf_op jit(solution)/shard_map/ppermute | solution.py:83
  150.1 12.2 %collective-permute-start.32 = (f32[2048]{0:T(1024)S(1)}, f32[2048]{0:T(1024)S(1)}, u32[]{:S(2)}, u32[]{:S(2)}) collective-permute-start(f32[2048]{0:T(1024)S(1)} %add.82), channel_id=1, source_target_pairs={{0,4},{4,0},{1,5},{5,1},{2,6},{6,2},{3,7},{7,3},{8,12},{12,8},{9,1... | collective-permute-start | bytes 24584 | tf_op jit(solution)/shard_map/ppermute | solution.py:120
  152.7 9.6 %collective-permute-start.31 = (bf16[2,64,384]{2,1,0:T(8,128)(2,1)S(1)}, bf16[2,64,384]{2,1,0:T(8,128)(2,1)S(1)}, u32[]{:S(2)}, u32[]{:S(2)}) collective-permute-start(bf16[2,64,384]{2,1,0:T(8,128)(2,1)S(1)} %slice.219), channel_id=1, source_target_pairs={{0,6},{1,3},{2,4},{3,1},{4,2},{5,7},{6,0},{7,5},{64,70},{65,67},{6... | collective-permute-start | bytes 294920 | tf_op jit(solution)/shard_map/ppermute | solution.py:83
  152.9 9.4 %collective-permute-start.30 = (bf16[2,64,512]{2,1,0:T(8,128)(2,1)S(1)}, bf16[2,64,512]{2,1,0:T(8,128)(2,1)S(1)}, u32[]{:S(2)}, u32[]{:S(2)}) collective-permute-start(bf16[2,64,512]{2,1,0:T(8,128)(2,1)S(1)} %slice.218), channel_id=1, source_target_pairs={{0,64},{1,193},{2,66},{3,195},{4,68},{5,197},{6,70},{7,199},{64,0}... | collective-permute-start | bytes 393224 | tf_op jit(solution)/shard_map/ppermute | solution.py:83
  162.4 8.9 %collective-permute-start.35 = (f32[2048]{0:T(1024)S(1)}, f32[2048]{0:T(1024)S(1)}, u32[]{:S(2)}, u32[]{:S(2)}) collective-permute-start(f32[2048]{0:T(1024)S(1)} %add.85), channel_id=1, source_target_pairs={{0,2},{2,0},{1,3},{3,1},{4,6},{6,4},{5,7},{7,5},{8,10},{10,8},{9,1... | collective-permute-start | bytes 24584 | tf_op jit(solution)/shard_map/ppermute | solution.py:120
  163.2 8.1 %collective-permute-start.34 = (bf16[1,64,384]{2,1,0:T(8,128)(2,1)S(1)}, bf16[1,64,384]{2,1,0:T(8,128)(2,1)S(1)}, u32[]{:S(2)}, u32[]{:S(2)}) collective-permute-start(bf16[1,64,384]{2,1,0:T(8,128)(2,1)S(1)} %slice.221), channel_id=1, source_target_pairs={{0,64},{1,193},{2,66},{3,195},{4,68},{5,197},{6,70},{7,199},{64,0}... | collective-permute-start | bytes 147464 | tf_op jit(solution)/shard_map/ppermute | solution.py:83
  164.2 7.2 %collective-permute-start.33 = (bf16[1,64,512]{2,1,0:T(8,128)(2,1)S(1)}, bf16[1,64,512]{2,1,0:T(8,128)(2,1)S(1)}, u32[]{:S(2)}, u32[]{:S(2)}) collective-permute-start(bf16[1,64,512]{2,1,0:T(8,128)(2,1)S(1)} %slice.220), channel_id=1, source_target_pairs={{0,2},{1,7},{2,0},{3,5},{4,6},{5,3},{6,4},{7,1},{64,66},{65,71},{6... | collective-permute-start | bytes 196616 | tf_op jit(solution)/shard_map/ppermute | solution.py:83
  164.4 19.8 %collective-permute-start.19 = (bf16[32,2048]{1,0:T(8,128)(2,1)S(1)}, bf16[32,2048]{1,0:T(8,128)(2,1)S(1)}, u32[]{:S(2)}, u32[]{:S(2)}) collective-permute-start(bf16[32,2048]{1,0:T(8,128)(2,1)S(1)} %fusion.5), channel_id=1, source_target_pairs={{0,0},{8,1},{16,2},{24,3},{4,4},{12,5},{20,6},{28,7},{32,8},{40,9}... | collective-permute-start | bytes 393224 | tf_op jit(solution)/shard_map/ppermute | solution.py:61
  171.4 14.2 %collective-permute-start.38 = (bf16[32,896]{1,0:T(8,128)(2,1)S(1)}, bf16[32,896]{1,0:T(8,128)(2,1)S(1)}, u32[]{:S(2)}, u32[]{:S(2)}) collective-permute-start(bf16[32,896]{1,0:T(8,128)(2,1)S(1)} %get-tuple-element.79), channel_id=1, source_target_pairs={{16,0},{48,1},{24,2},{56,3},{0,4},{32,5},{8,6},{40,7},{17,8},{49,9... | collective-permute-start | bytes 172040 | tf_op jit(solution)/shard_map/ppermute | solution.py:61
  174.2 11.4 %collective-permute-start.39 = (bf16[32,896]{1,0:T(8,128)(2,1)S(1)}, bf16[32,896]{1,0:T(8,128)(2,1)S(1)}, u32[]{:S(2)}, u32[]{:S(2)}) collective-permute-start(bf16[32,896]{1,0:T(8,128)(2,1)S(1)} %get-tuple-element.80), channel_id=1, source_target_pairs={{0,0},{32,1},{8,2},{40,3},{16,4},{48,5},{24,6},{56,7},{1,8},{33,9}... | collective-permute-start | bytes 172040 | tf_op jit(solution)/shard_map/ppermute | solution.py:61
  (22 other events, 260.0 us)
